TPU v7x, 8 devices: a whole 2x2x1 slice. The times are simulated.
8 devices in a mesh: ey: 4 (over z, y, x), ex: 2 (over core).
Axes of the slice: x: 2, y: 2, z: 1, core: 2. Of those that a mesh axis runs over, the one named last changes fastest.
Arguments:
- x: bfloat16 [512, 2048], P(('ey', 'ex'))
- kv_k: bfloat16 [512, 256, 4, 128], P(('ey', 'ex'))
- kv_v: bfloat16 [512, 256, 4, 128], P(('ey', 'ex'))
- lens: int32 [512], P(('ey', 'ex'))
- topk_idx: int32 [512, 8], P(('ey', 'ex'))
- gates: float32 [512, 8], P(('ey', 'ex'))
- ln1: bfloat16 [2048], replicated
- wq: bfloat16 [2048, 4096], replicated
- wo: bfloat16 [4096, 2048], replicated
- ln2: bfloat16 [2048], replicated
- ws1: bfloat16 [2048, 768], replicated
- ws3: bfloat16 [2048, 768], replicated
- ws2: bfloat16 [768, 2048], replicated
- w1: bfloat16 [128, 2048, 768], P(('ey', 'ex'))
- w3: bfloat16 [128, 2048, 768], P(('ey', 'ex'))
- w2: bfloat16 [128, 768, 2048], P(('ey', 'ex'))
Outputs:
- output: bfloat16 [512, 2048], P(('ey', 'ex'))
All inputs are finite; a program needn't handle non-finite values.
Results may differ from a plain program's by a relative error of at most 0.0116285.
Values are sent between devices in bfloat16 or wider.
A program may use at most 1 GiB of HBM per device.

v0:
```python
import jax
import jax.numpy as jnp
from jax import lax
from jax.sharding import PartitionSpec as P

EPS = 1e-6
GRP = ("ey", "ex")


def _rms(v, w):
    v32 = v.astype(jnp.float32)
    r = lax.rsqrt(jnp.mean(v32 * v32, axis=-1, keepdims=True) + EPS)
    return (v32 * r * w.astype(jnp.float32)).astype(jnp.bfloat16)


def _swiglu(a, w1, w3, w2):
    z1 = jnp.dot(a, w1, preferred_element_type=jnp.float32)
    z3 = jnp.dot(a, w3, preferred_element_type=jnp.float32)
    g = (jax.nn.silu(z1) * z3).astype(jnp.bfloat16)
    return jnp.dot(g, w2, preferred_element_type=jnp.float32)


def _experts(buf, w1, w3, w2):
    z1 = jnp.einsum("eqd,edf->eqf", buf, w1, preferred_element_type=jnp.float32)
    z3 = jnp.einsum("eqd,edf->eqf", buf, w3, preferred_element_type=jnp.float32)
    g = (jax.nn.silu(z1) * z3).astype(jnp.bfloat16)
    return jnp.einsum("eqf,efd->eqd", g, w2, preferred_element_type=jnp.float32).astype(jnp.bfloat16)


def _attention_block(x, kv_k, kv_v, lens, ln1, wq, wo):
    b, d = x.shape
    _, l, kvh, hd = kv_k.shape
    nh = wq.shape[1] // hd
    a = _rms(x, ln1)
    q = jnp.dot(a, wq, preferred_element_type=jnp.float32).astype(jnp.bfloat16).reshape(b, kvh, nh // kvh, hd)
    s = jnp.einsum("bkgh,blkh->bkgl", q, kv_k, preferred_element_type=jnp.float32) * hd ** -0.5
    s = jnp.where(jnp.arange(l) < lens[:, None, None, None], s, -jnp.inf)
    p = jax.nn.softmax(s, axis=-1).astype(jnp.bfloat16)
    o = jnp.einsum("bkgl,blkh->bkgh", p, kv_v, preferred_element_type=jnp.float32).astype(jnp.bfloat16)
    attn = jnp.dot(o.reshape(b, nh * hd), wo, preferred_element_type=jnp.float32)
    return (x.astype(jnp.float32) + attn).astype(jnp.bfloat16)


def solution(mesh):
    nx = mesh.shape["ex"]
    ndev = mesh.shape["ey"] * nx

    def body(x, kv_k, kv_v, lens, idx, gates, ln1, wq, wo, ln2, ws1, ws3, ws2, w1, w3, w2):
        bdev, d = x.shape
        top = idx.shape[1]
        edev = w1.shape[0]
        cap = bdev - bdev // 8
        rlen = min(bdev * top, edev * cap)
        qrows = ndev * cap
        my = lax.axis_index("ey") * nx + lax.axis_index("ex")
        h = _attention_block(x, kv_k, kv_v, lens, ln1, wq, wo)
        u = _rms(h, ln2)
        shared = _swiglu(u, ws1, ws3, ws2)
        flat = idx.reshape(-1)
        oh = jax.nn.one_hot(flat, edev * ndev, dtype=jnp.int32)
        rank = jnp.sum((jnp.cumsum(oh, axis=0) - oh) * oh, axis=1)
        keep = rank < cap
        dest = flat // edev
        ohd = jax.nn.one_hot(dest, ndev, dtype=jnp.int32) * keep.astype(jnp.int32)[:, None]
        slot = jnp.sum((jnp.cumsum(ohd, axis=0) - ohd) * ohd, axis=1)
        pos = jnp.where(keep, dest * rlen + slot, ndev * rlen)
        tok = jnp.arange(bdev * top) // top
        send_tok = jnp.full((ndev * rlen,), bdev, jnp.int32).at[pos].set(tok, mode="drop")
        send_rows = jnp.take(u, send_tok, axis=0, mode="fill", fill_value=0).reshape(ndev, rlen, d)
        meta = ((flat % edev) * ndev + my) * cap + rank
        send_meta = jnp.full((ndev * rlen,), edev * qrows, jnp.int32).at[pos].set(meta, mode="drop").reshape(ndev, rlen)
        recv_rows = lax.all_to_all(send_rows, GRP, 0, 0, tiled=True)
        recv_meta = lax.all_to_all(send_meta, GRP, 0, 0, tiled=True).reshape(-1)
        buf = jnp.zeros((edev * qrows, d), jnp.bfloat16).at[recv_meta].set(recv_rows.reshape(-1, d), mode="drop")
        out = _experts(buf.reshape(edev, qrows, d), w1, w3, w2).reshape(edev * qrows, d)
        back = jnp.take(out, recv_meta, axis=0, mode="fill", fill_value=0).reshape(ndev, rlen, d)
        ret = lax.all_to_all(back, GRP, 0, 0, tiled=True).reshape(ndev * rlen, d)
        e_rows = jnp.take(ret, pos, axis=0, mode="fill", fill_value=0).reshape(bdev, top, d)
        routed = jnp.sum(gates[:, :, None] * e_rows.astype(jnp.float32), axis=1)
        return (h.astype(jnp.float32) + shared + routed).astype(jnp.bfloat16)

    rows = P(GRP)
    rep = P()
    return jax.shard_map(
        body, mesh=mesh,
        in_specs=(rows, rows, rows, rows, rows, rows, rep, rep, rep, rep, rep, rep, rep, rows, rows, rows),
        out_specs=rows, check_vma=False)
```

profile of v0, /device:TPU:0, one launch (start us, length us, event | category | flops | bytes accessed | tf_op | source)
XLA Modules:
  0.0 766.5 jit_solution(11489087757326109605)
XLA Ops:
  0.0 0.9 copy.61
  0.9 0.1 eq.66
  1.0 0.1 eq.62
  1.1 0.1 copy.63
  1.3 0.1 reshape.311
  1.3 0.2 fusion.36
  1.7 0.2 fusion.35
  1.9 1.1 reduce-window.16
  3.1 0.2 slice_reduce_fusion
  3.4 0.1 fusion.47
  3.5 0.6 copy-done.5
  4.1 3.0 scatter_custom_fusion
  7.1 4.3 all-to-all-start
  11.4 2.6 scatter_custom_fusion.1
  14.1 0.7 convert_element_type.71
  14.8 1.1 fusion.28
  15.9 9.0 %fusion.22 = bf16[8,8,32,128]{3,1,2,0:T(8,128)(2,1)S(1)} fusion(bf16[2048,4096]{1,0:T(8,128)(2,1)} %param.23, bf16[64,2048]{1,0:T(8,128)(2,1)} %param.16, f32[2048]{0:T(1024)S(1)} %convert_element_type.71, f32[64]{0:T(128)S(1)} %add_rsqrt_fusion.1), kind=kOutput, calls=%fused_computation.35 | convolution fusion | flops 1074528256 | bytes 17572096 | tf_op jit(solution)/shard_map/dot_general | solution.py:35
  24.9 0.9 copy.70
  25.8 0.1 iota_compare_fusion.3
  25.9 11.9 %fusion.74 = (f32[64,4,8]{2,1,0:T(4,128)S(1)}, f32[64,4,8,256]{3,2,1,0:T(8,128)}) fusion(pred[64,256]{1,0:T(8,128)(4,1)S(1)} %iota_compare_fusion.3, bf16[64,4,8,128]{3,2,1,0:T(8,128)(2,1)} %bitcast.78, bf16[64,256,4,128]{3,2,1,0:T(4,128)(2,1)} %param.17), kind=kOutput, calls=%fused_computation.142 | convolution fusion | flops 136315136 | bytes 19423232 | tf_op jit(solution)/shard_map/sub | solution.py:38
  37.8 8.8 %fusion.19 = bf16[64,4,8,128]{3,2,1,0:T(8,128)(2,1)S(1)} fusion(bf16[64,256,4,128]{3,2,1,0:T(4,128)(2,1)} %param.18, f32[64,4,8,256]{3,2,1,0:T(8,128)} %get-tuple-element.12, f32[64,4,8]{2,1,0:T(4,128)S(1)} %get-tuple-element.11), kind=kOutput, calls=%fused_computation.34 | convolution fusion | flops 135528448 | bytes 19406848 | tf_op jit(solution)/shard_map/bkgl,blkh->bkgh/dot_general | solution.py:39
  46.6 9.7 %multiply_reduce_fusion.1 = (f32[64]{0:T(128)S(1)}, f32[64,2048]{1,0:T(8,128)}) fusion(bf16[4096,2048]{1,0:T(8,128)(2,1)} %param.24, bf16[8,8,32,128]{3,2,1,0:T(8,128)(2,1)S(1)} %bitcast.77, bf16[64,2048]{1,0:T(8,128)(2,1)S(1)} %copy-done.3), kind=kOutput, calls=%fused_computation.50 | convolution fusion | flops 1074528256 | bytes 18088192 | tf_op jit(solution)/shard_map/dot_general | solution.py:40
  56.3 1.2 multiply_convert_fusion.2
  57.5 21.0 %gather_fusion = bf16[4096,2048]{1,0:T(8,128)(2,1)} fusion(bf16[64,2048]{1,0:T(8,128)(2,1)S(1)} %multiply_convert_fusion.2, s32[4096]{0:T(1024)S(1)} %fusion.49), kind=kCustom, calls=%fused_computation | custom fusion | bytes 33570816 | tf_op jit(solution)/shard_map/jit(_take)/gather | solution.py:69
  78.5 14.0 %broadcast_select_fusion = bf16[8,512,2048]{2,1,0:T(8,128)(2,1)} fusion(bf16[8,512,2048]{2,1,0:T(8,128)(2,1)} %bitcast.72, pred[8,512]{1,0:T(8,128)(4,1)S(1)} %broadcast_in_dim.81), kind=kLoop, calls=%fused_computation.16 | loop fusion | flops 8388608 | bytes 33558528 | tf_op jit(solution)/shard_map/jit(_take)/select_n | solution.py:69
  92.5 4.9 all-to-all-start.1
  97.5 5.1 sort
  102.6 0.6 compare_and_fusion.1
  103.2 0.6 broadcast_clamp_fusion
  103.8 177.6 %all-to-all-done.1 = bf16[8,512,2048]{2,1,0:T(8,128)(2,1)} async-done(((bf16[8,512,2048]{2,1,0:T(8,128)(2,1)}), bf16[8,512,2048]{2,1,0:T(8,128)(2,1)}, u32[]{:S(2)}, u32[]{:S(2)}) %all-to-all-start.1) | async-done | bytes 16777248 | tf_op jit(solution)/shard_map/all_to_all | solution.py:72
  281.4 94.0 %scatter_custom_fusion.2 = bf16[7168,2048]{1,0:T(8,128)(2,1)} fusion(s32[4096]{0:T(1024)S(1)} %get-tuple-element.5, bf16[4096,2048]{1,0:T(8,128)(2,1)} %bitcast.12, s32[4096]{0:T(1024)S(1)} %broadcast_clamp_fusion.1, bf16[]{:T(256)} %constant.129.clone.1), kind=kCustom, calls=%fused_computation.10 | custom fusion | bytes 29360640 | tf_op jit(solution)/shard_map/scatter | solution.py:74
  375.4 39.3 %fusion.80 = f32[16,448,768]{2,1,0:T(8,128)} fusion(bf16[16,448,2048]{2,1,0:T(8,128)(2,1)} %bitcast.73, bf16[16,2048,768]{2,1,0:T(8,128)(2,1)} %param.29), kind=kOutput, calls=%fused_computation.144 | convolution fusion | flops 22548578304 | bytes 101711872 | tf_op jit(solution)/shard_map/eqd,edf->eqf/dot_general | solution.py:24
  414.7 45.5 %multiply_convert_fusion.5 = bf16[16,448,768]{2,1,0:T(8,128)(2,1)} fusion(f32[16,448,768]{2,1,0:T(8,128)} %fusion.80, bf16[16,448,2048]{2,1,0:T(8,128)(2,1)} %bitcast.74, bf16[16,2048,768]{2,1,0:T(8,128)(2,1)} %param.30), kind=kOutput, calls=%fused_computation.8.clone.clone.1 | convolution fusion | flops 22581608448 | bytes 112721920 | tf_op jit(solution)/shard_map/eqd,edf->eqf/dot_general | solution.py:25
  460.1 36.4 %convolution_convert_fusion = bf16[16,448,2048]{2,1,0:T(8,128)(2,1)} fusion(bf16[16,768,2048]{2,1,0:T(8,128)(2,1)} %param.31, bf16[16,448,768]{2,1,0:T(8,128)(2,1)} %multiply_convert_fusion.5), kind=kOutput, calls=%fused_computation.9 | convolution fusion | flops 22563258368 | bytes 90701824 | tf_op jit(solution)/shard_map/eqf,efd->eqd/dot_general | solution.py:27
  496.5 44.4 %gather_fusion.1 = bf16[4096,2048]{1,0:T(8,128)(2,1)} fusion(bf16[7168,2048]{1,0:T(8,128)(2,1)} %bitcast.70, s32[4096]{0:T(1024)S(1)} %copy-done.4), kind=kCustom, calls=%fused_computation.1 | custom fusion | bytes 33570816 | tf_op jit(solution)/shard_map/jit(_take)/gather | solution.py:76
  541.0 14.0 %broadcast_select_fusion.1 = bf16[8,512,2048]{2,1,0:T(8,128)(2,1)} fusion(bf16[8,512,2048]{2,1,0:T(8,128)(2,1)} %bitcast.71, pred[8,512]{1,0:T(8,128)(4,1)S(1)} %copy-done.7), kind=kLoop, calls=%fused_computation.17 | loop fusion | flops 8388608 | bytes 33558528 | tf_op jit(solution)/shard_map/jit(_take)/select_n | solution.py:76
  555.0 4.9 all-to-all-start.2
  560.0 0.1 reduce_sum.63
  560.1 0.1 lt.104
  560.2 0.1 copy.65
  560.2 0.1 copy.66
  560.3 0.1 copy.67
  560.4 0.1 copy.60
  560.6 3.2 fusion.79
  563.8 180.1 %all-to-all-done.2 = bf16[8,512,2048]{2,1,0:T(8,128)(2,1)} async-done(((bf16[8,512,2048]{2,1,0:T(8,128)(2,1)}), bf16[8,512,2048]{2,1,0:T(8,128)(2,1)}, u32[]{:S(2)}, u32[]{:S(2)}) %all-to-all-start.2) | async-done | bytes 16777248 | tf_op jit(solution)/shard_map/all_to_all | solution.py:77
  743.9 13.2 %gather_fusion.2 = bf16[512,2048]{1,0:T(8,128)(2,1)} fusion(bf16[4096,2048]{1,0:T(8,128)(2,1)} %bitcast.16, s32[1024]{0:T(1024)S(1)} %pad_clamp_fusion), kind=kCustom, calls=%fused_computation.2 | custom fusion | bytes 4196352 | tf_op jit(solution)/shard_map/jit(_take)/gather | solution.py:78
  757.1 4.7 multiply_reduce_fusion
  761.8 4.3 fusion.17
  (58 shorter events, 0.4 us)
Async XLA Ops:
  0.0 761.8 %copy-start = (bf16[768,2048]{1,0:T(8,128)(2,1)S(1)}, bf16[768,2048]{1,0:T(8,128)(2,1)}, u32[]{:S(2)}) copy-start(bf16[768,2048]{1,0:T(8,128)(2,1)} %param.28) | copy-start | bytes 9437188
  0.0 25.8 %copy-start.15 = (s32[64]{0:T(128)S(1)}, s32[64]{0:T(128)}, u32[]{:S(2)}) copy-start(s32[64]{0:T(128)} %param.19) | copy-start | bytes 772
  1.9 35.9 %copy-start.11 = (pred[512]{0:T(512)(128)(4,1)}, pred[512]{0:T(512)(128)(4,1)S(1)}, u32[]{:S(2)}) copy-start(pred[512]{0:T(512)(128)(4,1)S(1)} %get-tuple-element.8) | copy-start | bytes 1540
  3.5 0.6 copy-start.5
  4.1 10.0 %copy-start.9 = (s32[512,1]{0,1:T(1,128)}, s32[512,1]{0,1:T(1,128)S(1)}, u32[]{:S(2)}) copy-start(s32[512,1]{0,1:T(1,128)S(1)} %compare_select_fusion.3) | copy-start | bytes 6148
  7.1 85.4 %all-to-all-start = ((s32[8,1,512]{2,1,0:T(1,128)}), s32[8,1,512]{2,1,0:T(1,128)S(1)}, u32[]{:S(2)}, u32[]{:S(2)}) async-start(s32[8,1,512]{2,1,0:T(1,128)} %bitcast.8), calls=%async_computation | async-start | bytes 32768 | tf_op jit(solution)/shard_map/all_to_all | solution.py:73
  37.8 8.8 %copy-start.3 = (bf16[64,2048]{1,0:T(8,128)(2,1)S(1)}, bf16[64,2048]{1,0:T(8,128)(2,1)}, u32[]{:S(2)}) copy-start(bf16[64,2048]{1,0:T(8,128)(2,1)} %param.16) | copy-start | bytes 786436
  46.6 9.7 %copy-start.13 = (bf16[2048]{0:T(1024)(128)(2,1)S(1)}, bf16[2048]{0:T(1024)(128)(2,1)}, u32[]{:S(2)}) copy-start(bf16[2048]{0:T(1024)(128)(2,1)} %param.25) | copy-start | bytes 12292
  57.5 21.0 %copy-start.1 = (bf16[64,2048]{1,0:T(8,128)(2,1)}, bf16[64,2048]{1,0:T(8,128)(2,1)S(1)}, u32[]{:S(2)}) copy-start(bf16[64,2048]{1,0:T(8,128)(2,1)S(1)} %multiply_convert_fusion.2) | copy-start | bytes 786436
  92.5 188.9 %all-to-all-start.1 = ((bf16[8,512,2048]{2,1,0:T(8,128)(2,1)}), bf16[8,512,2048]{2,1,0:T(8,128)(2,1)}, u32[]{:S(2)}, u32[]{:S(2)}) async-start(bf16[8,512,2048]{2,1,0:T(8,128)(2,1)} %broadcast_select_fusion), calls=%async_computation.1 | async-start | bytes 33554432 | tf_op jit(solution)/shard_map/all_to_all | solution.py:72
  460.1 36.4 %copy-start.4 = (s32[4096]{0:T(1024)S(1)}, s32[4096]{0:T(1024)}, u32[]{:S(2)}) copy-start(s32[4096]{0:T(1024)} %broadcast_clamp_fusion) | copy-start | bytes 49156
  496.5 44.5 %copy-start.7 = (pred[8,512]{1,0:T(8,128)(4,1)S(1)}, pred[8,512]{1,0:T(8,128)(4,1)}, u32[]{:S(2)}) copy-start(pred[8,512]{1,0:T(8,128)(4,1)} %compare_and_fusion.1) | copy-start | bytes 12292
  555.0 5.0 copy-start.6
  555.0 5.1 copy-start.12
  555.0 5.3 copy-start.8
  555.0 5.5 copy-start.14
  555.0 5.5 copy-start.10
  555.0 5.6 copy-start.2
  555.0 188.9 %all-to-all-start.2 = ((bf16[8,512,2048]{2,1,0:T(8,128)(2,1)}), bf16[8,512,2048]{2,1,0:T(8,128)(2,1)}, u32[]{:S(2)}, u32[]{:S(2)}) async-start(bf16[8,512,2048]{2,1,0:T(8,128)(2,1)} %broadcast_select_fusion.1), calls=%async_computation.2 | async-start | bytes 33554432 | tf_op jit(solution)/shard_map/all_to_all | solution.py:77
where the time goes:
time: 771 us; the launch traced here: 766 us
  waiting for transfers between devices  358 us (46%)
  local copies, waits for them, and re-layouts  182 us (24%)
  matrix products  168 us (22%)
  other arithmetic  44 us (6%)
  starting transfers between devices  14.1 us (2%)
    all_to_all x1, waiting for transfers between devices, body(): ret = lax.all_to_all(back, GRP, 0, 0, tiled=True).reshape(ndev * rlen, d)  180 us
    all_to_all x1, waiting for transfers between devices, body(): recv_rows = lax.all_to_all(send_rows, GRP, 0, 0, tiled=True)  178 us
    scatter x2, local copies, waits for them, and re-layouts, body(): jnp.zeros((edev * qrows, d), jnp.bfloat16).at[recv_meta]  94 us
    dot_general x1, matrix products, _experts(): z3 = jnp.einsum('eqd,edf->eqf', buf, w3, preferred_element_type=jnp.float32)  45.5 us
    gather x1, local copies, waits for them, and re-layouts, body(): jnp.take(out, recv_meta, axis=0, mode='fill', fill_value=0)  44.4 us
    dot_general x1, matrix products, _experts(): z1 = jnp.einsum('eqd,edf->eqf', buf, w1, preferred_element_type=jnp.float32)  39.3 us
    dot_general x1, matrix products, _experts(): jnp.einsum('eqf,efd->eqd', g, w2, preferred_element_type=jnp.float32)  36.4 us
    gather x1, local copies, waits for them, and re-layouts, body(): jnp.take(u, send_tok, axis=0, mode='fill', fill_value=0)  21 us
  transfers between devices with their start and end apart: 3, of which 2 were waited for; matrix products, arithmetic and copies ran while one was open for 12% of the time, Pallas kernels for 0%

commit v1 on v0

v1 whole, which is shorter than its diff:
```python
import functools

import jax
import jax.numpy as jnp
from jax import lax
from jax.experimental import pallas as pl
from jax.experimental.pallas import tpu as pltpu
from jax.sharding import PartitionSpec as P

EPS = 1e-6
GRP = ("ey", "ex")
MESH = pl.DeviceIdType.MESH
NEG = -1e30
F32 = jnp.float32
BF16 = jnp.bfloat16
VLIM = 62 * 1024 * 1024


def _vm():
    return pl.BlockSpec(memory_space=pltpu.VMEM)


def _sm():
    return pl.BlockSpec(memory_space=pltpu.SMEM)


def _any():
    return pl.BlockSpec(memory_space=pl.ANY)


def _rms(v, w):
    v32 = v.astype(F32)
    r = lax.rsqrt(jnp.mean(v32 * v32, axis=-1, keepdims=True) + EPS)
    return (v32 * r * w.astype(F32)).astype(BF16)


SEQ = 4
KVBUF = 6
STEP = 64


def _attn_kernel(lens, x, ln1, ln2, idx, gates, kk, vv, wq, wo, h_out, u_out, pk_out,
                 wqb, wob, kb, vb, qs, os, ob, bias, hf, wq_sem, wo_sem, k_sem, v_sem):
    b, d = x.shape
    heads_dim = wqb.shape[1]
    hd = 128
    nh = heads_dim // hd
    rows = kk.shape[1]
    kvh = 4
    seqlen = rows // kvh
    ncls = seqlen // STEP
    crow = STEP * kvh
    ngrp = b // SEQ
    nwq = wq_sem.shape[0]
    nwo = wo_sem.shape[0]
    cq = heads_dim // nwq
    co = d // nwo

    def wq_copy(i):
        c = pl.ds(pl.multiple_of(i * cq, cq), cq)
        return pltpu.make_async_copy(wq.at[:, c], wqb.at[:, c], wq_sem.at[i])

    def wo_copy(i):
        c = pl.ds(pl.multiple_of(i * co, co), co)
        return pltpu.make_async_copy(wo.at[:, c], wob.at[:, c], wo_sem.at[i])

    def gmax(g):
        m = lens[g * SEQ]
        for s in range(1, SEQ):
            m = jnp.maximum(m, lens[g * SEQ + s])
        return m

    def kv_copies(g, slot, n):
        src = (pl.ds(g * SEQ, SEQ), pl.ds(0, n * crow))
        dst = (slot, slice(None), pl.ds(0, n * crow))
        return (pltpu.make_async_copy(kk.at[src], kb.at[dst], k_sem.at[slot]),
                pltpu.make_async_copy(vv.at[src], vb.at[dst], v_sem.at[slot]))

    def by_class(g, f):
        cls = (gmax(g) + STEP - 1) // STEP
        for n in range(1, ncls + 1):
            pl.when(cls == n)(functools.partial(f, n))

    def start_kv(g):
        slot = lax.rem(g, KVBUF)

        def go(n):
            for c in kv_copies(g, slot, n):
                c.start()
        by_class(g, go)

    for i in range(nwq):
        wq_copy(i).start()
    lax.fori_loop(0, min(KVBUF, ngrp), lambda g, _: (start_kv(g), 0)[1], 0)
    for i in range(nwo // 2):
        wo_copy(i).start()

    pk_out[...] = jnp.concatenate(
        [idx[...].astype(F32), gates[...], jnp.zeros((b, 128 - 2 * idx.shape[1]), F32)], axis=1)
    col = lax.broadcasted_iota(jnp.int32, (nh, rows), 1)
    row = lax.broadcasted_iota(jnp.int32, (nh, rows), 0)
    bias[...] = jnp.where(lax.rem(col, kvh) == row // (nh // kvh), 0.0, NEG)

    a = _rms(x[...], ln1[...])

    def qstep(i, _):
        wq_copy(i).wait()
        w = wqb[:, pl.ds(pl.multiple_of(i * cq, cq), cq)]
        q = jnp.dot(a, w, preferred_element_type=F32).astype(BF16).astype(F32)
        for j in range(cq // hd):
            qs[pl.ds(i * (cq // hd) + j, b, stride=nh), :] = q[:, j * hd:(j + 1) * hd]
        return 0

    lax.fori_loop(0, nwq, qstep, 0)
    for i in range(nwo // 2, nwo):
        wo_copy(i).start()

    def group(g, _):
        slot = lax.rem(g, KVBUF)

        def go(n):
            for c in kv_copies(g, slot, n):
                c.wait()
            w = n * crow
            lane = lax.broadcasted_iota(jnp.int32, (nh, w), 1)
            for s in range(SEQ):
                sb = g * SEQ + s
                r = pl.ds(pl.multiple_of(sb * nh, nh), nh)
                q = qs[r, :].astype(BF16)
                k = kb[slot, s, 0:w, :]
                sc = lax.dot_general(q, k, (((1,), (1,)), ((), ())), preferred_element_type=F32)
                sc = sc * (hd ** -0.5) + bias[:, 0:w]
                sc = jnp.where(lane < lens[sb] * kvh, sc, NEG)
                m = jnp.max(sc, axis=1, keepdims=True)
                p = jnp.exp(sc - m)
                p = (p / jnp.sum(p, axis=1, keepdims=True)).astype(BF16)
                o = jnp.dot(p, vb[slot, s, 0:w, :], preferred_element_type=F32)
                os[r, :] = o.astype(BF16).astype(F32)
        by_class(g, go)
        pl.when(g + KVBUF < ngrp)(lambda: start_kv(g + KVBUF))
        return 0

    lax.fori_loop(0, ngrp, group, 0)

    for j in range(nh):
        ob[:, j * hd:(j + 1) * hd] = os[pl.ds(j, b, stride=nh), :].astype(BF16)

    def ostep(i, _):
        wo_copy(i).wait()
        c = pl.ds(pl.multiple_of(i * co, co), co)
        attn = jnp.dot(ob[...], wob[:, c], preferred_element_type=F32)
        hf[:, c] = (x[:, c].astype(F32) + attn).astype(BF16)
        return 0

    lax.fori_loop(0, nwo, ostep, 0)
    h = hf[...]
    h_out[...] = h
    u_out[...] = _rms(h, ln2[...])


def _attention(x, kv_k, kv_v, lens, idx, gates, ln1, ln2, wq, wo):
    b, d = x.shape
    _, l, kvh, hd = kv_k.shape
    hdim = wq.shape[1]
    nh = hdim // hd
    rows = l * kvh
    kk = kv_k.reshape(b, rows, hd)
    vv = kv_v.reshape(b, rows, hd)
    return pl.pallas_call(
        _attn_kernel,
        name="attn",
        out_shape=(jax.ShapeDtypeStruct((b, d), BF16), jax.ShapeDtypeStruct((b, d), BF16),
                   jax.ShapeDtypeStruct((b, 128), F32)),
        in_specs=[_sm(), _vm(), _vm(), _vm(), _vm(), _vm(), _any(), _any(), _any(), _any()],
        out_specs=(_vm(), _vm(), _vm()),
        scratch_shapes=[
            pltpu.VMEM((d, hdim), BF16),
            pltpu.VMEM((hdim, d), BF16),
            pltpu.VMEM((KVBUF, SEQ, rows, hd), BF16),
            pltpu.VMEM((KVBUF, SEQ, rows, hd), BF16),
            pltpu.VMEM((b * nh, hd), F32),
            pltpu.VMEM((b * nh, hd), F32),
            pltpu.VMEM((b, hdim), BF16),
            pltpu.VMEM((nh, rows), F32),
            pltpu.VMEM((b, d), BF16),
            pltpu.SemaphoreType.DMA((8,)),
            pltpu.SemaphoreType.DMA((8,)),
            pltpu.SemaphoreType.DMA((KVBUF,)),
            pltpu.SemaphoreType.DMA((KVBUF,)),
        ],
        compiler_params=pltpu.CompilerParams(vmem_limit_bytes=VLIM),
    )(lens, x, ln1.reshape(1, d), ln2.reshape(1, d), idx, gates, kk, vv, wq, wo)


def _places():
    cy = lax.axis_index("ey")
    cx = lax.axis_index("ex")
    xn = cy + 1 - 2 * lax.rem(cy, 2)
    yn = lax.rem(cy + 2, 4)
    dg = 3 - cy
    return cy, cx, (xn, yn, dg)


def _barrier(cy, cx, others):
    bar = pltpu.get_barrier_semaphore()
    for o in others:
        pl.semaphore_signal(bar, inc=1, device_id=(o, cx), device_id_type=MESH)
    pl.semaphore_signal(bar, inc=1, device_id=(cy, 1 - cx), device_id_type=MESH)
    pl.semaphore_wait(bar, len(others) + 1)


def _gather_kernel(u, pk, ua, pka, s_sem, r_sem, fs_sem, fr_sem):
    cy, cx, others = _places()
    _barrier(cy, cx, others)
    me = 2 * cy + cx

    def both(src_u, src_p, slot, dev, ss, rs, i):
        return (
            pltpu.make_async_remote_copy(
                src_ref=src_u, dst_ref=ua.at[slot], send_sem=ss.at[0, i], recv_sem=rs.at[0, i],
                device_id=dev, device_id_type=MESH),
            pltpu.make_async_remote_copy(
                src_ref=src_p, dst_ref=pka.at[slot], send_sem=ss.at[1, i], recv_sem=rs.at[1, i],
                device_id=dev, device_id_type=MESH))

    sends = []
    for i in (2, 0, 1):
        sends.append((i, both(u, pk, me, (others[i], cx), s_sem, r_sem, i)))
    for _, cs in sends:
        for c in cs:
            c.start()
    mine = both(u, pk, me, (cy, 1 - cx), fs_sem, fr_sem, 3)
    for c in mine:
        c.start()
    ua[me] = u[...]
    pka[me] = pk[...]
    fwds = [mine]
    for i in (0, 1, 2):
        slot = 2 * others[i] + cx
        for c in both(u, pk, slot, (others[i], cx), s_sem, r_sem, i):
            c.wait_recv()
        f = both(ua.at[slot], pka.at[slot], slot, (cy, 1 - cx), fs_sem, fr_sem, i)
        for c in f:
            c.start()
        fwds.append(f)
    for f in fwds:
        for c in f:
            c.wait()
    for _, cs in sends:
        for c in cs:
            c.wait_send()


def _all_gather(u, pk):
    b, d = u.shape
    return pl.pallas_call(
        _gather_kernel,
        name="gather",
        out_shape=(jax.ShapeDtypeStruct((8, b, d), BF16), jax.ShapeDtypeStruct((8, b, 128), F32)),
        in_specs=[_vm(), _vm()],
        out_specs=(_vm(), _vm()),
        scratch_shapes=[
            pltpu.SemaphoreType.DMA((2, 3)),
            pltpu.SemaphoreType.DMA((2, 3)),
            pltpu.SemaphoreType.DMA((2, 4)),
            pltpu.SemaphoreType.DMA((2, 4)),
        ],
        compiler_params=pltpu.CompilerParams(collective_id=0, has_side_effects=True),
    )(u, pk)


TILE = 128
WBUF = 4


def _silu_mul(z1, z3):
    return (z1 * jax.nn.sigmoid(z1) * z3).astype(BF16)


def _expert_kernel(first, ua, pka, h, u, ws1, ws3, ws2, w1, w3, w2, acc, hs,
                   b1, b3, b2, tmap, posk, posb, gateb, xt, gt, rt, cnt, sem):
    ntok, d = ua.shape
    ne = w1.shape[0]
    f = w1.shape[2]
    top = 8
    blk = ntok // 8
    cap = blk - blk // 8
    fc = 256
    dc = 512

    def copies(e, slot):
        return (pltpu.make_async_copy(w1.at[e], b1.at[slot], sem.at[0, slot]),
                pltpu.make_async_copy(w3.at[e], b3.at[slot], sem.at[1, slot]),
                pltpu.make_async_copy(w2.at[e], b2.at[slot], sem.at[2, slot]))

    shared = (pltpu.make_async_copy(ws1, b1.at[WBUF - 1], sem.at[0, WBUF - 1]),
              pltpu.make_async_copy(ws3, b3.at[WBUF - 1], sem.at[1, WBUF - 1]),
              pltpu.make_async_copy(ws2, b2.at[WBUF - 1], sem.at[2, WBUF - 1]))
    for c in shared:
        c.start()
    for e in range(WBUF - 1):
        for c in copies(e, e):
            c.start()

    e0 = first[0]
    tmap[...] = jnp.transpose(pka[...])
    ids = e0 + lax.broadcasted_iota(jnp.int32, (ne, ntok), 0)
    ids = ids.astype(F32)
    member = jnp.zeros((ne, ntok), F32)
    gate = jnp.zeros((ne, ntok), F32)
    for j in range(top):
        hit = tmap[j:j + 1, :] == ids
        member = member + jnp.where(hit, 1.0, 0.0)
        gate = gate + jnp.where(hit, tmap[top + j:top + j + 1, :], 0.0)
    ti = lax.broadcasted_iota(jnp.int32, (ntok, ntok), 0)
    tj = lax.broadcasted_iota(jnp.int32, (ntok, ntok), 1)
    tri = ti < tj
    tri_b = (tri & (ti // blk == tj // blk)).astype(F32).astype(BF16)
    rank = jnp.dot(member.astype(BF16), tri_b, preferred_element_type=F32)
    keep = jnp.where(rank < cap, member, 0.0)
    pos = jnp.dot(keep.astype(BF16), tri.astype(F32).astype(BF16), preferred_element_type=F32)
    pk = jnp.where(keep > 0, pos, -1.0)
    gk = gate * keep
    posk[...] = pk
    for e in range(ne):
        cnt[e] = jnp.sum(keep[e:e + 1, :]).astype(jnp.int32)
    both = jnp.concatenate([pk, gk, jnp.zeros((128 - 2 * ne, ntok), F32)], axis=0)
    cols = jnp.transpose(both)
    for e in range(ne):
        posb[e] = jnp.broadcast_to(cols[:, e:e + 1], (ntok, 128))
        gateb[e] = jnp.broadcast_to(cols[:, ne + e:ne + e + 1], (ntok, 128))

    def zero(i, _):
        acc[pl.ds(pl.multiple_of(i * 64, 64), 64), :] = jnp.zeros((64, d), F32)
        return 0
    lax.fori_loop(0, ntok // 64, zero, 0)

    for c in shared:
        c.wait()
    for c in range(f // fc):
        s = slice(c * fc, (c + 1) * fc)
        z1 = jnp.dot(u[...], b1[WBUF - 1, :, s], preferred_element_type=F32)
        z3 = jnp.dot(u[...], b3[WBUF - 1, :, s], preferred_element_type=F32)
        gt[0:blk, s] = _silu_mul(z1, z3)
    for c in range(d // dc):
        s = slice(c * dc, (c + 1) * dc)
        hs[:, s] = h[:, s].astype(F32) + jnp.dot(gt[0:blk, :], b2[WBUF - 1, :, s], preferred_element_type=F32)
    for c in copies(WBUF - 1, WBUF - 1):
        c.start()

    def ffn(slot):
        for c in range(f // fc):
            s = slice(c * fc, (c + 1) * fc)
            z1 = jnp.dot(xt[...], b1[slot, :, s], preferred_element_type=F32)
            z3 = jnp.dot(xt[...], b3[slot, :, s], preferred_element_type=F32)
            gt[:, s] = _silu_mul(z1, z3)
        for c in range(d // dc):
            s = slice(c * dc, (c + 1) * dc)
            rt[:, s] = jnp.dot(gt[...], b2[slot, :, s], preferred_element_type=F32).astype(BF16)

    def expert(e, _):
        slot = lax.rem(e, WBUF)
        for c in copies(e, slot):
            c.wait()
        n = cnt[e]

        def packed(t, _):
            base = t * TILE
            want = (lax.broadcasted_iota(jnp.int32, (TILE, ntok), 0) + base).astype(F32)
            sel = (posk[pl.ds(e, 1), :] == want).astype(F32).astype(BF16)
            for c in range(d // dc):
                s = slice(c * dc, (c + 1) * dc)
                xt[:, s] = jnp.dot(sel, ua[:, s], preferred_element_type=F32).astype(BF16)
            ffn(slot)
            wantc = (lax.broadcasted_iota(jnp.int32, (ntok, TILE), 1) + base).astype(F32)
            selt = (posb[e] == wantc).astype(F32).astype(BF16)
            for c in range(d // 256):
                s = slice(c * 256, (c + 1) * 256)
                y = jnp.dot(selt, rt[:, s], preferred_element_type=F32)
                g = gateb[e]
                acc[:, c * 256:c * 256 + 128] += g * y[:, 0:128]
                acc[:, c * 256 + 128:(c + 1) * 256] += g * y[:, 128:256]
            return 0

        def dense(t, _):
            rows = pl.ds(pl.multiple_of(t * TILE, TILE), TILE)
            xt[...] = ua[rows, :]
            ffn(slot)
            g = gateb[e, rows, :]
            for c in range(d // 128):
                s = slice(c * 128, (c + 1) * 128)
                acc[rows, s] += g * rt[:, s].astype(F32)
            return 0

        many = n > 2 * TILE
        lax.fori_loop(0, jnp.where(many, 0, (n + TILE - 1) // TILE), packed, 0)
        lax.fori_loop(0, jnp.where(many, ntok // TILE, 0), dense, 0)

        @pl.when(e + WBUF < ne)
        def _():
            for c in copies(e + WBUF, slot):
                c.start()
        return 0

    lax.fori_loop(0, ne, expert, 0)


def _experts(first, ua, pka, h, u, ws1, ws3, ws2, w1, w3, w2):
    ntok, d = ua.shape
    b = u.shape[0]
    ne, _, f = w1.shape
    return pl.pallas_call(
        _expert_kernel,
        name="experts",
        out_shape=(jax.ShapeDtypeStruct((ntok, d), F32), jax.ShapeDtypeStruct((b, d), F32)),
        in_specs=[_sm(), _vm(), _vm(), _vm(), _vm()] + [_any()] * 6,
        out_specs=(_vm(), _vm()),
        scratch_shapes=[
            pltpu.VMEM((WBUF, d, f), BF16),
            pltpu.VMEM((WBUF, d, f), BF16),
            pltpu.VMEM((WBUF, f, d), BF16),
            pltpu.VMEM((128, ntok), F32),
            pltpu.VMEM((ne, ntok), F32),
            pltpu.VMEM((ne, ntok, 128), F32),
            pltpu.VMEM((ne, ntok, 128), F32),
            pltpu.VMEM((TILE, d), BF16),
            pltpu.VMEM((TILE, f), BF16),
            pltpu.VMEM((TILE, d), BF16),
            pltpu.SMEM((ne,), jnp.int32),
            pltpu.SemaphoreType.DMA((3, WBUF)),
        ],
        compiler_params=pltpu.CompilerParams(vmem_limit_bytes=VLIM),
    )(first, ua, pka, h, u, ws1, ws3, ws2, w1, w3, w2)


CH = 4


def _return_kernel(acc, hs, y, rbuf, sbuf, gbuf, ds_sem, dr_sem, s_sem, r_sem):
    cy, cx, others = _places()
    _barrier(cy, cx, others)
    d = acc.shape[3]
    w = d // CH

    def cols(c):
        return pl.ds(c * w, w)

    def pair(c):
        return pltpu.make_async_remote_copy(
            src_ref=acc.at[:, 1 - cx, :, cols(c)], dst_ref=rbuf.at[c], send_sem=ds_sem.at[c], recv_sem=dr_sem.at[c],
            device_id=(cy, 1 - cx), device_id_type=MESH)

    def far(c, i):
        return pltpu.make_async_remote_copy(
            src_ref=sbuf.at[c, others[i]], dst_ref=gbuf.at[c, i], send_sem=s_sem.at[c, i], recv_sem=r_sem.at[c, i],
            device_id=(others[i], cx), device_id_type=MESH)

    for c in range(CH):
        pair(c).start()
    for c in range(CH):
        pair(c).wait_recv()
        for k in range(4):
            sbuf[c, k] = acc[k, cx, :, c * w:(c + 1) * w] + rbuf[c, k]
        for i in (2, 0, 1):
            far(c, i).start()
    for c in range(CH):
        for i in range(3):
            far(c, i).wait_recv()
        s = slice(c * w, (c + 1) * w)
        t = hs[:, s] + sbuf[c, cy]
        t = t + (gbuf[c, 0] + gbuf[c, 1] + gbuf[c, 2])
        y[:, s] = t.astype(BF16)
    for c in range(CH):
        pair(c).wait_send()
        for i in range(3):
            far(c, i).wait_send()


def _return(acc, hs):
    b, d = hs.shape
    w = d // CH
    return pl.pallas_call(
        _return_kernel,
        name="giveback",
        out_shape=jax.ShapeDtypeStruct((b, d), BF16),
        in_specs=[_vm(), _vm()],
        out_specs=_vm(),
        scratch_shapes=[
            pltpu.VMEM((CH, 4, b, w), F32),
            pltpu.VMEM((CH, 4, b, w), F32),
            pltpu.VMEM((CH, 3, b, w), F32),
            pltpu.SemaphoreType.DMA((CH,)),
            pltpu.SemaphoreType.DMA((CH,)),
            pltpu.SemaphoreType.DMA((CH, 3)),
            pltpu.SemaphoreType.DMA((CH, 3)),
        ],
        compiler_params=pltpu.CompilerParams(collective_id=1, has_side_effects=True, vmem_limit_bytes=VLIM),
    )(acc, hs)


def solution(mesh):
    nx = mesh.shape["ex"]

    def body(x, kv_k, kv_v, lens, idx, gates, ln1, wq, wo, ln2, ws1, ws3, ws2, w1, w3, w2):
        b, d = x.shape
        edev = w1.shape[0]
        me = lax.axis_index("ey") * nx + lax.axis_index("ex")
        h, u, pk = _attention(x, kv_k, kv_v, lens, idx, gates, ln1, ln2, wq, wo)
        ua, pka = _all_gather(u, pk)
        first = (me * edev).astype(jnp.int32).reshape(1)
        acc, hs = _experts(first, ua.reshape(8 * b, d), pka.reshape(8 * b, 128), h, u, ws1, ws3, ws2, w1, w3, w2)
        return _return(acc.reshape(4, 2, b, d), hs)

    rows = P(GRP)
    rep = P()
    return jax.shard_map(
        body, mesh=mesh,
        in_specs=(rows, rows, rows, rows, rows, rows, rep, rep, rep, rep, rep, rep, rep, rows, rows, rows),
        out_specs=rows, check_vma=False)
```

time: 771 us -> 162 us (0.21)
  waiting for transfers between devices: 358 us -> 0 us
  local copies, waits for them, and re-layouts: 182 us -> 7.01 us
  matrix products: 168 us -> 0 us
  Pallas kernels: 0 us -> 155 us
  other arithmetic: 44 us -> 0 us
  starting transfers between devices: 14.1 us -> 0 us
    all_to_all x3 -> x0, waiting for transfers between devices: 358 us -> none  [the longest x1 180 us: body(): ret = lax.all_to_all(back, GRP, 0, 0, tiled=True).reshape(ndev * rlen, d)]
    dot_general x8 -> x0, matrix products: 156 us -> none  [the longest x1 45.5 us: _experts(): z3 = jnp.einsum('eqd,edf->eqf', buf, w3, preferred_element_type=jnp.float32)]
    pallas_call x0 -> x4, Pallas kernels: none -> 155 us  [the longest x1 54.1 us: _experts(): pl.pallas_call(_expert_kernel, name='experts', out_shape=(jax.ShapeDtypeS...]
    scatter x4 -> x0, local copies, waits for them, and re-layouts: 99.7 us -> none  [the longest x2 94 us: body(): jnp.zeros((edev * qrows, d), jnp.bfloat16).at[recv_meta]]
    gather x3 -> x0, local copies, waits for them, and re-layouts: 78.7 us -> none  [the longest x1 44.4 us: body(): jnp.take(out, recv_meta, axis=0, mode='fill', fill_value=0)]
    select_n x6 -> x0, other arithmetic: 28.1 us -> none  [the longest x2 14 us: body(): jnp.take(out, recv_meta, axis=0, mode='fill', fill_value=0)]
    all_to_all x3 -> x0, starting transfers between devices: 14.1 us -> none  [the longest x1 4.93 us: body(): ret = lax.all_to_all(back, GRP, 0, 0, tiled=True).reshape(ndev * rlen, d)]
    sub x1 -> x0, matrix products: 11.9 us -> none  [_attention_block(): p = jax.nn.softmax(s, axis=-1).astype(jnp.bfloat16)]
  transfers between devices with their start and end apart: 3 -> 0, of which waited for: 2 -> 0; matrix products, arithmetic and copies ran while one was open for 12% -> 0% of each run, Pallas kernels for 0% -> 0%
where the time goes in v1:
time: 162 us
  Pallas kernels  155 us (96%)
  local copies, waits for them, and re-layouts  7.01 us (4%)
    pallas_call x1, Pallas kernels, _experts(): pl.pallas_call(_expert_kernel, name='experts', out_shape=(jax.ShapeDtypeS...  54.1 us
    pallas_call x1, Pallas kernels, _attention(): pl.pallas_call(_attn_kernel, name='attn', out_shape=(jax.ShapeDtypeStruct...  42.2 us
    pallas_call x1, Pallas kernels, _return(): pl.pallas_call(_return_kernel, name='giveback', out_shape=jax.ShapeDtypeS...  39.7 us
    pallas_call x1, Pallas kernels, _all_gather(): pl.pallas_call(_gather_kernel, name='gather', out_shape=(jax.ShapeDtypeSt...  18.5 us
    unnamed x3, local copies, waits for them, and re-layouts  4.44 us

profile of v1, /device:TPU:0, one launch (start us, length us, event | category | flops | bytes accessed | tf_op | source)
XLA Modules:
  0.0 161.6 jit_solution(4427517384569484084)
XLA Ops:
  0.0 1.3 reshape.25.ln1
  1.3 1.3 reshape.26.ln2
  2.6 1.4 copy.17.idx
  4.0 1.4 copy.18.gates
  5.3 42.2 %attn.1 = (bf16[64,2048]{1,0:T(8,128)(2,1)}, bf16[64,2048]{1,0:T(8,128)(2,1)}, f32[64,128]{1,0:T(8,128)}) custom-call(s32[64]{0:T(128)} %lens.1, bf16[64,2048]{1,0:T(8,128)(2,1)} %x.1, bf16[1,2048]{1,0:T(2,128)(2,1)} %reshape.25.ln1, bf16[1,2048]{1,0:T(2,128)(2,1)} %reshape.26.ln2, s32[64,8]{1,0:T(8,128)} %copy.17.idx, f32[64,8]{1,0:T(8,128)} %copy.18.gates, ...), custom_call_target="tpu_custom_call" | custom-call | tf_op jit(solution)/shard_map/attn/pallas_call | solution.py:169
  47.6 18.5 %gather.1 = (bf16[8,64,2048]{2,1,0:T(8,128)(2,1)}, f32[8,64,128]{2,1,0:T(8,128)}) custom-call(bf16[64,2048]{1,0:T(8,128)(2,1)} %get-tuple-element.12.u, f32[64,128]{1,0:T(8,128)} %get-tuple-element.13.pk), custom_call_target="tpu_custom_call" | custom-call | tf_op jit(solution)/shard_map/gather/pallas_call | solution.py:256
  66.1 54.1 %experts.1 = (f32[512,2048]{1,0:T(8,128)}, f32[64,2048]{1,0:T(8,128)}) custom-call(s32[1]{0:T(128)} %bitcast.first, bf16[512,2048]{1,0:T(8,128)(2,1)} %bitcast.9, f32[512,128]{1,0:T(8,128)} %bitcast.10, bf16[64,2048]{1,0:T(8,128)(2,1)} %get-tuple-element.16.h, bf16[64,2048]{1,0:T(8,128)(2,1)} %get-tuple-element.12.u, bf16[2048,768]{1,0:T(8,128)(2,1)} %ws1.1, ...), custom_call_target="tpu_custom_call" | custom-call | tf_op jit(solution)/shard_map/experts/pallas_call | solution.py:412
  120.2 39.7 %giveback.1 = bf16[64,2048]{1,0:T(8,128)(2,1)} custom-call(f32[4,2,64,2048]{3,2,1,0:T(8,128)} %bitcast.8, f32[64,2048]{1,0:T(8,128)} %get-tuple-element.18.hs), custom_call_target="tpu_custom_call" | custom-call | tf_op jit(solution)/shard_map/giveback/pallas_call | solution.py:482
  159.9 1.7 %copy.20 = bf16[64,2048]{1,0:T(8,128)(2,1)} copy(bf16[64,2048]{1,0:T(8,128)(2,1)} %giveback.1) | data formatting | bytes 524288

commit v2 on v1

v2 whole, which is shorter than its diff:
```python
import functools

import jax
import jax.numpy as jnp
from jax import lax
from jax.experimental import pallas as pl
from jax.experimental.pallas import tpu as pltpu
from jax.sharding import PartitionSpec as P

EPS = 1e-6
GRP = ("ey", "ex")
MESH = pl.DeviceIdType.MESH
NEG = -1e30
F32 = jnp.float32
BF16 = jnp.bfloat16
VLIM = 55 * 1024 * 1024


def _vm():
    return pl.BlockSpec(memory_space=pltpu.VMEM)


def _sm():
    return pl.BlockSpec(memory_space=pltpu.SMEM)


def _any():
    return pl.BlockSpec(memory_space=pl.ANY)


def _rms(v, w):
    v32 = v.astype(F32)
    r = lax.rsqrt(jnp.mean(v32 * v32, axis=-1, keepdims=True) + EPS)
    return (v32 * r * w.astype(F32)).astype(BF16)


SEQ = 8
KVBUF = 4
STEP = 64


def _attn_kernel(lens, x, ln1, ln2, idx, gates, kk, vv, wq, wo, h_out, u_out, pk_out,
                 wqb, wob, kb, vb, qs, os, ob, bias, hf, ss, ps, wq_sem, wo_sem, k_sem, v_sem):
    b, d = x.shape
    heads_dim = wqb.shape[1]
    hd = 128
    nh = heads_dim // hd
    rows = kk.shape[1]
    kvh = 4
    seqlen = rows // kvh
    ncls = seqlen // STEP
    crow = STEP * kvh
    ngrp = b // SEQ
    nwq = wq_sem.shape[0]
    nwo = wo_sem.shape[0]
    cq = heads_dim // nwq
    co = d // nwo

    def wq_copy(i):
        c = pl.ds(pl.multiple_of(i * cq, cq), cq)
        return pltpu.make_async_copy(wq.at[:, c], wqb.at[:, c], wq_sem.at[i])

    def wo_copy(i):
        c = pl.ds(pl.multiple_of(i * co, co), co)
        return pltpu.make_async_copy(wo.at[:, c], wob.at[:, c], wo_sem.at[i])

    def gmax(g):
        m = lens[g * SEQ]
        for s in range(1, SEQ):
            m = jnp.maximum(m, lens[g * SEQ + s])
        return m

    def kv_copies(g, slot, n):
        src = (pl.ds(g * SEQ, SEQ), pl.ds(0, n * crow))
        dst = (slot, slice(None), pl.ds(0, n * crow))
        return (pltpu.make_async_copy(kk.at[src], kb.at[dst], k_sem.at[slot]),
                pltpu.make_async_copy(vv.at[src], vb.at[dst], v_sem.at[slot]))

    def by_class(g, f):
        cls = (gmax(g) + STEP - 1) // STEP
        for n in range(1, ncls + 1):
            pl.when(cls == n)(functools.partial(f, n))

    def start_kv(g):
        slot = lax.rem(g, KVBUF)

        def go(n):
            for c in kv_copies(g, slot, n):
                c.start()
        by_class(g, go)

    for i in range(nwq):
        wq_copy(i).start()
    lax.fori_loop(0, min(KVBUF, ngrp), lambda g, _: (start_kv(g), 0)[1], 0)
    table = jnp.concatenate([idx[...].astype(F32), gates[...]], axis=0)
    table = jnp.concatenate([table, jnp.zeros((table.shape[0], 128 - b), F32)], axis=1)
    table = jnp.concatenate([table, jnp.zeros((128 - table.shape[0], 128), F32)], axis=0)
    pk_out[...] = jnp.transpose(table)[0:b, :]
    col = lax.broadcasted_iota(jnp.int32, (nh, rows), 1)
    row = lax.broadcasted_iota(jnp.int32, (nh, rows), 0)
    bias[...] = jnp.where(lax.rem(col, kvh) == row // (nh // kvh), 0.0, NEG)

    a = _rms(x[...], ln1[...])

    def qstep(i, _):
        wq_copy(i).wait()
        w = wqb[:, pl.ds(pl.multiple_of(i * cq, cq), cq)]
        q = jnp.dot(a, w, preferred_element_type=F32).astype(BF16).astype(F32)
        for j in range(cq // hd):
            qs[pl.ds(i * (cq // hd) + j, b, stride=nh), :] = q[:, j * hd:(j + 1) * hd]
        return 0

    lax.fori_loop(0, nwq, qstep, 0)
    per = nwo // min(KVBUF, ngrp)

    def group(g, _):
        slot = lax.rem(g, KVBUF)

        def go(n):
            for c in kv_copies(g, slot, n):
                c.wait()
            w = n * crow
            lane = lax.broadcasted_iota(jnp.int32, (nh, w), 1)
            rq = [pl.ds(pl.multiple_of((g * SEQ + s) * nh, nh), nh) for s in range(SEQ)]
            for s in range(SEQ):
                q = qs[rq[s], :].astype(BF16)
                k = kb[slot, s, 0:w, :]
                ss[s * nh:(s + 1) * nh, 0:w] = lax.dot_general(
                    q, k, (((1,), (1,)), ((), ())), preferred_element_type=F32)
            for s in range(SEQ):
                sc = ss[s * nh:(s + 1) * nh, 0:w] * (hd ** -0.5) + bias[:, 0:w]
                sc = jnp.where(lane < lens[g * SEQ + s] * kvh, sc, NEG)
                m = jnp.max(sc, axis=1, keepdims=True)
                p = jnp.exp(sc - m)
                ps[s * nh:(s + 1) * nh, 0:w] = (p * (1.0 / jnp.sum(p, axis=1, keepdims=True))).astype(BF16)
            for s in range(SEQ):
                o = jnp.dot(ps[s * nh:(s + 1) * nh, 0:w], vb[slot, s, 0:w, :], preferred_element_type=F32)
                os[rq[s], :] = o.astype(BF16).astype(F32)
        by_class(g, go)
        pl.when(g + KVBUF < ngrp)(lambda: start_kv(g + KVBUF))

        @pl.when(g + KVBUF >= ngrp)
        def _():
            for i in range(per):
                wo_copy((g + KVBUF - ngrp) * per + i).start()
        return 0

    lax.fori_loop(0, ngrp, group, 0)

    for j in range(nh):
        ob[:, j * hd:(j + 1) * hd] = os[pl.ds(j, b, stride=nh), :].astype(BF16)

    def ostep(i, _):
        wo_copy(i).wait()
        c = pl.ds(pl.multiple_of(i * co, co), co)
        attn = jnp.dot(ob[...], wob[:, c], preferred_element_type=F32)
        hf[:, c] = (x[:, c].astype(F32) + attn).astype(BF16)
        return 0

    lax.fori_loop(0, nwo, ostep, 0)
    h = hf[...]
    h_out[...] = h
    u_out[...] = _rms(h, ln2[...])


def _attention(x, kv_k, kv_v, lens, idx, gates, ln1, ln2, wq, wo):
    b, d = x.shape
    _, l, kvh, hd = kv_k.shape
    hdim = wq.shape[1]
    nh = hdim // hd
    rows = l * kvh
    kk = kv_k.reshape(b, rows, hd)
    vv = kv_v.reshape(b, rows, hd)
    return pl.pallas_call(
        _attn_kernel,
        name="attn",
        out_shape=(pltpu.VMEM((b, d), BF16), pltpu.VMEM((b, d), BF16), pltpu.VMEM((b, 128), F32)),
        in_specs=[_sm(), _vm(), _vm(), _vm(), _vm(), _vm(), _any(), _any(), _any(), _any()],
        out_specs=(_vm(), _vm(), _vm()),
        scratch_shapes=[
            pltpu.VMEM((d, hdim), BF16),
            pltpu.VMEM((hdim, d), BF16),
            pltpu.VMEM((KVBUF, SEQ, rows, hd), BF16),
            pltpu.VMEM((KVBUF, SEQ, rows, hd), BF16),
            pltpu.VMEM((b * nh, hd), F32),
            pltpu.VMEM((b * nh, hd), F32),
            pltpu.VMEM((b, hdim), BF16),
            pltpu.VMEM((nh, rows), F32),
            pltpu.VMEM((b, d), BF16),
            pltpu.VMEM((SEQ * nh, rows), F32),
            pltpu.VMEM((SEQ * nh, rows), BF16),
            pltpu.SemaphoreType.DMA((8,)),
            pltpu.SemaphoreType.DMA((8,)),
            pltpu.SemaphoreType.DMA((KVBUF,)),
            pltpu.SemaphoreType.DMA((KVBUF,)),
        ],
        compiler_params=pltpu.CompilerParams(vmem_limit_bytes=VLIM),
    )(lens, x, ln1, ln2, idx.T, gates.T, kk, vv, wq, wo)


def _places():
    cy = lax.axis_index("ey")
    cx = lax.axis_index("ex")
    xn = cy + 1 - 2 * lax.rem(cy, 2)
    yn = lax.rem(cy + 2, 4)
    dg = 3 - cy
    return cy, cx, (xn, yn, dg)


def _barrier(cy, cx, others):
    bar = pltpu.get_barrier_semaphore()
    for o in others:
        pl.semaphore_signal(bar, inc=1, device_id=(o, cx), device_id_type=MESH)
    pl.semaphore_signal(bar, inc=1, device_id=(cy, 1 - cx), device_id_type=MESH)
    pl.semaphore_wait(bar, len(others) + 1)


WBUF = 4
TILE = 128


def _silu_mul(z1, z3):
    return (z1 * jax.nn.sigmoid(z1) * z3).astype(BF16)


def _slot_copies(w1, w3, w2, b1, b3, b2, sem, e, slot):
    return (pltpu.make_async_copy(w1.at[e], b1.at[slot], sem.at[0, slot]),
            pltpu.make_async_copy(w3.at[e], b3.at[slot], sem.at[1, slot]),
            pltpu.make_async_copy(w2.at[e], b2.at[slot], sem.at[2, slot]))


def _gather_kernel(u, pk, h, ws1, ws3, ws2, w1, w3, w2, ua, posk, cols, hs, b1, b3, b2,
                   pka, v1, v3, v2, gt, tmap, s_sem, r_sem, fs_sem, fr_sem, w_sem, v_sem):
    blk, d = u.shape
    ntok = 8 * blk
    ne = w1.shape[0]
    f = w1.shape[2]
    top = 8
    cap = blk - blk // 8
    cy, cx, others = _places()
    me = 2 * cy + cx

    shared = (pltpu.make_async_copy(ws1, v1, v_sem.at[0]),
              pltpu.make_async_copy(ws3, v3, v_sem.at[1]),
              pltpu.make_async_copy(ws2, v2, v_sem.at[2]))
    for c in shared:
        c.start()
    ahead = [_slot_copies(w1, w3, w2, b1, b3, b2, w_sem, e, e) for e in range(WBUF)]
    for cs in ahead:
        for c in cs:
            c.start()

    _barrier(cy, cx, others)

    def pair(k, src, slot, dev, ss, rs, i):
        out = (ua, pka)[k]
        return pltpu.make_async_remote_copy(
            src_ref=src, dst_ref=out.at[slot], send_sem=ss.at[k, i], recv_sem=rs.at[k, i],
            device_id=dev, device_id_type=MESH)

    src = (u, pk)
    outs = (ua, pka)
    for k in (1, 0):
        for i in (2, 0, 1):
            pair(k, src[k], me, (others[i], cx), s_sem, r_sem, i).start()
        pair(k, src[k], me, (cy, 1 - cx), fs_sem, fr_sem, 3).start()
    ua[me] = u[...]
    pka[me] = pk[...]

    for c in shared:
        c.wait()
    for c in range(f // 256):
        s = slice(c * 256, (c + 1) * 256)
        z1 = jnp.dot(u[...], v1[:, s], preferred_element_type=F32)
        z3 = jnp.dot(u[...], v3[:, s], preferred_element_type=F32)
        gt[:, s] = _silu_mul(z1, z3)
    for c in range(d // 512):
        s = slice(c * 512, (c + 1) * 512)
        hs[:, s] = h[:, s].astype(F32) + jnp.dot(gt[...], v2[:, s], preferred_element_type=F32)

    def relay(k):
        for i in (0, 1, 2):
            slot = 2 * others[i] + cx
            pair(k, src[k], slot, (others[i], cx), s_sem, r_sem, i).wait_recv()
            pair(k, outs[k].at[slot], slot, (cy, 1 - cx), fs_sem, fr_sem, i).start()

    def settle(k):
        for i in (0, 1, 2):
            slot = 2 * others[i] + cx
            pair(k, outs[k].at[slot], slot, (cy, 1 - cx), fs_sem, fr_sem, i).wait()
            pair(k, src[k], me, (others[i], cx), s_sem, r_sem, i).wait_send()
        pair(k, src[k], me, (cy, 1 - cx), fs_sem, fr_sem, 3).wait()

    relay(1)
    settle(1)

    tmap[...] = jnp.transpose(pka[...].reshape(ntok, 128))
    ids = (me * ne + lax.broadcasted_iota(jnp.int32, (ne, ntok), 0)).astype(F32)
    member = jnp.zeros((ne, ntok), F32)
    gate = jnp.zeros((ne, ntok), F32)
    for j in range(top):
        hit = tmap[j:j + 1, :] == ids
        member = member + jnp.where(hit, 1.0, 0.0)
        gate = gate + jnp.where(hit, tmap[top + j:top + j + 1, :], 0.0)
    ti = lax.broadcasted_iota(jnp.int32, (ntok, ntok), 0)
    tj = lax.broadcasted_iota(jnp.int32, (ntok, ntok), 1)
    tri = ti < tj
    tri_b = (tri & (ti // blk == tj // blk)).astype(F32).astype(BF16)
    rank = jnp.dot(member.astype(BF16), tri_b, preferred_element_type=F32)
    keep = jnp.where(rank < cap, member, 0.0)
    pos = jnp.dot(keep.astype(BF16), tri.astype(F32).astype(BF16), preferred_element_type=F32)
    pkeep = jnp.where(keep > 0, pos, -1.0)
    posk[...] = pkeep
    both = jnp.concatenate([pkeep, gate * keep, jnp.zeros((128 - 2 * ne, ntok), F32)], axis=0)
    cols[...] = jnp.transpose(both)

    relay(0)
    settle(0)
    for cs in ahead:
        for c in cs:
            c.wait()


def _all_gather(u, pk, h, ws1, ws3, ws2, w1, w3, w2):
    b, d = u.shape
    ne, _, f = w1.shape
    return pl.pallas_call(
        _gather_kernel,
        name="gather",
        out_shape=(pltpu.VMEM((8, b, d), BF16),
                   pltpu.VMEM((ne, 8 * b), F32),
                   pltpu.VMEM((8 * b, 128), F32),
                   pltpu.VMEM((b, d), F32),
                   pltpu.VMEM((WBUF, d, f), BF16),
                   pltpu.VMEM((WBUF, d, f), BF16),
                   pltpu.VMEM((WBUF, f, d), BF16)),
        in_specs=[_vm(), _vm(), _vm()] + [_any()] * 6,
        out_specs=(_vm(),) * 7,
        scratch_shapes=[
            pltpu.VMEM((8, b, 128), F32),
            pltpu.VMEM((d, f), BF16),
            pltpu.VMEM((d, f), BF16),
            pltpu.VMEM((f, d), BF16),
            pltpu.VMEM((b, f), BF16),
            pltpu.VMEM((128, 8 * b), F32),
            pltpu.SemaphoreType.DMA((2, 3)),
            pltpu.SemaphoreType.DMA((2, 3)),
            pltpu.SemaphoreType.DMA((2, 4)),
            pltpu.SemaphoreType.DMA((2, 4)),
            pltpu.SemaphoreType.DMA((3, WBUF)),
            pltpu.SemaphoreType.DMA((3,)),
        ],
        compiler_params=pltpu.CompilerParams(
            collective_id=0, has_side_effects=True, vmem_limit_bytes=12 * 1024 * 1024),
    )(u, pk, h, ws1, ws3, ws2, w1, w3, w2)


def _expert_kernel(ua, posk, cols, i1, i3, i2, w1, w3, w2, acc, b1, b3, b2, xt, gt, rt, psc, gsc, cnt, sem):
    del i1, i3, i2
    ntok, d = ua.shape
    ne = w1.shape[0]
    f = w1.shape[2]
    fc = 256
    dc = 512

    def copies(e, slot):
        return _slot_copies(w1, w3, w2, b1, b3, b2, sem, e, slot)

    for e in range(ne):
        cnt[e] = (jnp.max(posk[e:e + 1, :]) + 1.0).astype(jnp.int32)

    def zero(i, _):
        acc[pl.ds(pl.multiple_of(i * 64, 64), 64), :] = jnp.zeros((64, d), F32)
        return 0
    lax.fori_loop(0, ntok // 64, zero, 0)

    def ffn(slot):
        for c in range(f // fc):
            s = slice(c * fc, (c + 1) * fc)
            z1 = jnp.dot(xt[...], b1[slot, :, s], preferred_element_type=F32)
            z3 = jnp.dot(xt[...], b3[slot, :, s], preferred_element_type=F32)
            gt[:, s] = _silu_mul(z1, z3)
        for c in range(d // dc):
            s = slice(c * dc, (c + 1) * dc)
            rt[:, s] = jnp.dot(gt[...], b2[slot, :, s], preferred_element_type=F32).astype(BF16)

    def expert(e, _):
        slot = lax.rem(e, WBUF)

        @pl.when(e >= WBUF)
        def _():
            for c in copies(e, slot):
                c.wait()
        n = cnt[e]
        lane = lax.broadcasted_iota(jnp.int32, (ntok, 128), 1)
        psc[...] = jnp.broadcast_to(
            jnp.sum(jnp.where(lane == e, cols[...], 0.0), axis=1, keepdims=True), (ntok, 128))
        gsc[...] = jnp.broadcast_to(
            jnp.sum(jnp.where(lane == e + ne, cols[...], 0.0), axis=1, keepdims=True), (ntok, 128))

        def packed(t, _):
            base = t * TILE
            want = (lax.broadcasted_iota(jnp.int32, (TILE, ntok), 0) + base).astype(F32)
            sel = (posk[pl.ds(e, 1), :] == want).astype(F32).astype(BF16)
            for c in range(d // dc):
                s = slice(c * dc, (c + 1) * dc)
                xt[:, s] = jnp.dot(sel, ua[:, s], preferred_element_type=F32).astype(BF16)
            ffn(slot)
            wantc = (lax.broadcasted_iota(jnp.int32, (ntok, TILE), 1) + base).astype(F32)
            selt = (psc[...] == wantc).astype(F32).astype(BF16)
            for c in range(d // 256):
                s = slice(c * 256, (c + 1) * 256)
                y = jnp.dot(selt, rt[:, s], preferred_element_type=F32)
                g = gsc[...]
                acc[:, c * 256:c * 256 + 128] += g * y[:, 0:128]
                acc[:, c * 256 + 128:(c + 1) * 256] += g * y[:, 128:256]
            return 0

        def dense(t, _):
            rows = pl.ds(pl.multiple_of(t * TILE, TILE), TILE)
            xt[...] = ua[rows, :]
            ffn(slot)
            g = gsc[rows, :]
            for c in range(d // 128):
                s = slice(c * 128, (c + 1) * 128)
                acc[rows, s] += g * rt[:, s].astype(F32)
            return 0

        many = n > 2 * TILE
        lax.fori_loop(0, jnp.where(many, 0, (n + TILE - 1) // TILE), packed, 0)
        lax.fori_loop(0, jnp.where(many, ntok // TILE, 0), dense, 0)

        @pl.when(e + WBUF < ne)
        def _():
            for c in copies(e + WBUF, slot):
                c.start()
        return 0

    lax.fori_loop(0, ne, expert, 0)


def _experts(ua, posk, cols, i1, i3, i2, w1, w3, w2):
    ntok, d = ua.shape
    ne, _, f = w1.shape
    return pl.pallas_call(
        _expert_kernel,
        name="experts",
        out_shape=(pltpu.VMEM((ntok, d), F32),
                   pltpu.VMEM((WBUF, d, f), BF16),
                   pltpu.VMEM((WBUF, d, f), BF16),
                   pltpu.VMEM((WBUF, f, d), BF16)),
        in_specs=[_vm()] * 6 + [_any()] * 3,
        out_specs=(_vm(),) * 4,
        input_output_aliases={3: 1, 4: 2, 5: 3},
        scratch_shapes=[
            pltpu.VMEM((TILE, d), BF16),
            pltpu.VMEM((TILE, f), BF16),
            pltpu.VMEM((TILE, d), BF16),
            pltpu.VMEM((ntok, 128), F32),
            pltpu.VMEM((ntok, 128), F32),
            pltpu.SMEM((ne,), jnp.int32),
            pltpu.SemaphoreType.DMA((3, WBUF)),
        ],
        compiler_params=pltpu.CompilerParams(vmem_limit_bytes=3584 * 1024),
    )(ua, posk, cols, i1, i3, i2, w1, w3, w2)[0]


CH = 4


def _return_kernel(acc, hs, y, rbuf, sbuf, gbuf, ds_sem, dr_sem, s_sem, r_sem):
    cy, cx, others = _places()
    _barrier(cy, cx, others)
    d = acc.shape[3]
    w = d // CH

    def cols(c):
        return pl.ds(c * w, w)

    def pair(c):
        return pltpu.make_async_remote_copy(
            src_ref=acc.at[:, 1 - cx, :, cols(c)], dst_ref=rbuf.at[c], send_sem=ds_sem.at[c], recv_sem=dr_sem.at[c],
            device_id=(cy, 1 - cx), device_id_type=MESH)

    def far(c, i):
        return pltpu.make_async_remote_copy(
            src_ref=sbuf.at[c, others[i]], dst_ref=gbuf.at[c, i], send_sem=s_sem.at[c, i], recv_sem=r_sem.at[c, i],
            device_id=(others[i], cx), device_id_type=MESH)

    for c in range(CH):
        pair(c).start()
    for c in range(CH):
        pair(c).wait_recv()
        for k in range(4):
            sbuf[c, k] = acc[k, cx, :, c * w:(c + 1) * w] + rbuf[c, k]
        for i in (2, 0, 1):
            far(c, i).start()
    for c in range(CH):
        for i in range(3):
            far(c, i).wait_recv()
        s = slice(c * w, (c + 1) * w)
        t = hs[:, s] + sbuf[c, cy]
        t = t + (gbuf[c, 0] + gbuf[c, 1] + gbuf[c, 2])
        y[:, s] = t.astype(BF16)
    for c in range(CH):
        pair(c).wait_send()
        for i in range(3):
            far(c, i).wait_send()


def _return(acc, hs):
    b, d = hs.shape
    w = d // CH
    return pl.pallas_call(
        _return_kernel,
        name="giveback",
        out_shape=jax.ShapeDtypeStruct((b, d), BF16),
        in_specs=[_vm(), _vm()],
        out_specs=_vm(),
        scratch_shapes=[
            pltpu.VMEM((CH, 4, b, w), F32),
            pltpu.VMEM((CH, 4, b, w), F32),
            pltpu.VMEM((CH, 3, b, w), F32),
            pltpu.SemaphoreType.DMA((CH,)),
            pltpu.SemaphoreType.DMA((CH,)),
            pltpu.SemaphoreType.DMA((CH, 3)),
            pltpu.SemaphoreType.DMA((CH, 3)),
        ],
        compiler_params=pltpu.CompilerParams(
            collective_id=1, has_side_effects=True, vmem_limit_bytes=9 * 1024 * 1024),
    )(acc, hs)


def solution(mesh):
    def body(x, kv_k, kv_v, lens, idx, gates, ln1, wq, wo, ln2, ws1, ws3, ws2, w1, w3, w2):
        b, d = x.shape
        h, u, pk = _attention(x, kv_k, kv_v, lens, idx, gates, ln1, ln2, wq, wo)
        ua, posk, cols, hs, b1, b3, b2 = _all_gather(u, pk, h, ws1, ws3, ws2, w1, w3, w2)
        acc = _experts(ua.reshape(8 * b, d), posk, cols, b1, b3, b2, w1, w3, w2)
        return _return(acc.reshape(4, 2, b, d), hs)

    rows = P(GRP)
    rep = P()
    return jax.shard_map(
        body, mesh=mesh,
        in_specs=(rows, rows, rows, rows, rows, rows, rep, rep, rep, rep, rep, rep, rep, rows, rows, rows),
        out_specs=rows, check_vma=False)
```

time: 162 us -> 119 us (0.73)
  Pallas kernels: 155 us -> 118 us
  local copies, waits for them, and re-layouts: 7.01 us -> 0.71 us
    pallas_call x3, Pallas kernels: 115 us -> 83.9 us  [the longest x1 41.2 us: _experts(): pl.pallas_call(_expert_kernel, name='experts', out_shape=(pltpu.VMEM((nto...]
    pallas_call x1, Pallas kernels: 39.7 us -> 33.9 us  [_return(): pl.pallas_call(_return_kernel, name='giveback', out_shape=jax.ShapeDtypeS...]
    unnamed x3 -> x1, local copies, waits for them, and re-layouts: 4.44 us -> 0.71 us
    reshape x2 -> x0, local copies, waits for them, and re-layouts: 2.57 us -> none  [the longest x1 1.29 us: _attention(): ln2.reshape(1, d)]
where the time goes in v2:
time: 119 us; the launch traced here: 118 us
  Pallas kernels  118 us (99%)
    pallas_call x1, Pallas kernels, _experts(): pl.pallas_call(_expert_kernel, name='experts', out_shape=(pltpu.VMEM((nto...  41.2 us
    pallas_call x1, Pallas kernels, _return(): pl.pallas_call(_return_kernel, name='giveback', out_shape=jax.ShapeDtypeS...  33.9 us
    pallas_call x1, Pallas kernels, _attention(): pl.pallas_call(_attn_kernel, name='attn', out_shape=(pltpu.VMEM((b, d), B...  23.3 us
    pallas_call x1, Pallas kernels, _all_gather(): pl.pallas_call(_gather_kernel, name='gather', out_shape=(pltpu.VMEM((8, b...  19.4 us

profile of v2, /device:TPU:0, one launch (start us, length us, event | category | flops | bytes accessed | tf_op | source)
XLA Modules:
  0.0 118.5 jit_solution(9411214801630145601)
XLA Ops:
  0.0 23.3 %attn.1 = (bf16[64,2048]{1,0:T(8,128)(2,1)S(1)}, bf16[64,2048]{1,0:T(8,128)(2,1)S(1)}, f32[64,128]{1,0:T(8,128)S(1)}) custom-call(s32[64]{0:T(128)} %lens.1, bf16[64,2048]{1,0:T(8,128)(2,1)} %x.1, bf16[2048]{0:T(1024)(128)(2,1)} %ln1.1, bf16[2048]{0:T(1024)(128)(2,1)} %ln2.1, s32[8,64]{1,0:T(8,128)} %bitcast.10, f32[8,64]{1,0:T(8,128)} %bitcast.11, ...), custom_call_target="tpu_custom_call" | custom-call | tf_op jit(solution)/shard_map/attn/pallas_call | solution.py:174
  23.3 19.4 %gather.1 = (bf16[8,64,2048]{2,1,0:T(8,128)(2,1)S(1)}, f32[16,512]{1,0:T(8,128)S(1)}, f32[512,128]{1,0:T(8,128)S(1)}, f32[64,2048]{1,0:T(8,128)S(1)}, bf16[4,204...) custom-call(bf16[64,2048]{1,0:T(8,128)(2,1)S(1)} %get-tuple-element.16.u, ...), custom_call_target="tpu_custom_call" | custom-call | tf_op jit(solution)/shard_map/gather/pallas_call | solution.py:327
  42.7 41.2 %experts.1 = (f32[512,2048]{1,0:T(8,128)S(1)}, bf16[4,2048,768]{2,1,0:T(8,128)(2,1)S(1)}, bf16[4,2048,768]{2,1,0:T(8,128)(2,1)S(1)}, bf16[4,768,2048]{2,1,0:T(8,128)(2,1)S(1)}) custom-call(bf16[512,2048]{1,0:T(8,128)(2,1)S(1)} %bitcast.7, f32[16,512]{1,0:T(8,128)S(1)} %get-tuple-element.20.posk, ...), custom_call_target="tpu_custom_call", output_to_operand_aliasing={{1}: (3, {}), {2}: (4, {}), {3}: (5, {})} | custom-call | tf_op jit(solution)/shard_map/experts/pallas_call | solution.py:445
  83.9 33.9 %giveback.1 = bf16[64,2048]{1,0:T(8,128)(2,1)S(1)} custom-call(f32[4,2,64,2048]{3,2,1,0:T(8,128)S(1)} %bitcast.6, f32[64,2048]{1,0:T(8,128)S(1)} %get-tuple-element.26.hs), custom_call_target="tpu_custom_call" | custom-call | tf_op jit(solution)/shard_map/giveback/pallas_call | solution.py:514
  117.8 0.7 copy.24

commit v3 on v2

--- a/solution.py
+++ b/solution.py
@@ -22,6 +22,10 @@
 
 def _sm():
     return pl.BlockSpec(memory_space=pltpu.SMEM)
+
+
+def _hbm():
+    return pl.BlockSpec(memory_space=pltpu.HBM)
 
 
 def _any():
@@ -93,9 +97,7 @@
         wq_copy(i).start()
     lax.fori_loop(0, min(KVBUF, ngrp), lambda g, _: (start_kv(g), 0)[1], 0)
     table = jnp.concatenate([idx[...].astype(F32), gates[...]], axis=0)
-    table = jnp.concatenate([table, jnp.zeros((table.shape[0], 128 - b), F32)], axis=1)
-    table = jnp.concatenate([table, jnp.zeros((128 - table.shape[0], 128), F32)], axis=0)
-    pk_out[...] = jnp.transpose(table)[0:b, :]
+    pk_out[...] = jnp.concatenate([table, jnp.zeros((table.shape[0], 128 - b), F32)], axis=1)
     col = lax.broadcasted_iota(jnp.int32, (nh, rows), 1)
     row = lax.broadcasted_iota(jnp.int32, (nh, rows), 0)
     bias[...] = jnp.where(lax.rem(col, kvh) == row // (nh // kvh), 0.0, NEG)
@@ -174,7 +176,7 @@
     return pl.pallas_call(
         _attn_kernel,
         name="attn",
-        out_shape=(pltpu.VMEM((b, d), BF16), pltpu.VMEM((b, d), BF16), pltpu.VMEM((b, 128), F32)),
+        out_shape=(pltpu.VMEM((b, d), BF16), pltpu.VMEM((b, d), BF16), pltpu.VMEM((2 * idx.shape[1], 128), F32)),
         in_specs=[_sm(), _vm(), _vm(), _vm(), _vm(), _vm(), _any(), _any(), _any(), _any()],
         out_specs=(_vm(), _vm(), _vm()),
         scratch_shapes=[
@@ -229,22 +231,18 @@
             pltpu.make_async_copy(w2.at[e], b2.at[slot], sem.at[2, slot]))
 
 
-def _gather_kernel(u, pk, h, ws1, ws3, ws2, w1, w3, w2, ua, posk, cols, hs, b1, b3, b2,
-                   pka, v1, v3, v2, gt, tmap, s_sem, r_sem, fs_sem, fr_sem, w_sem, v_sem):
+def _gather_kernel(u, pk, w1, w3, w2, ua, posk, cols, b1, b3, b2,
+                   pka, tmap, ps_sem, pr_sem, s_sem, r_sem, fs_sem, fr_sem, os_sem, or_sem, w_sem):
     blk, d = u.shape
     ntok = 8 * blk
     ne = w1.shape[0]
-    f = w1.shape[2]
     top = 8
     cap = blk - blk // 8
+    half = blk // 2
     cy, cx, others = _places()
+    xn, yn, dg = others
     me = 2 * cy + cx
 
-    shared = (pltpu.make_async_copy(ws1, v1, v_sem.at[0]),
-              pltpu.make_async_copy(ws3, v3, v_sem.at[1]),
-              pltpu.make_async_copy(ws2, v2, v_sem.at[2]))
-    for c in shared:
-        c.start()
     ahead = [_slot_copies(w1, w3, w2, b1, b3, b2, w_sem, e, e) for e in range(WBUF)]
     for cs in ahead:
         for c in cs:
@@ -252,76 +250,96 @@
 
     _barrier(cy, cx, others)
 
-    def pair(k, src, slot, dev, ss, rs, i):
-        out = (ua, pka)[k]
+    def table(src, slot, dev, i):
         return pltpu.make_async_remote_copy(
-            src_ref=src, dst_ref=out.at[slot], send_sem=ss.at[k, i], recv_sem=rs.at[k, i],
+            src_ref=src, dst_ref=pka.at[slot], send_sem=ps_sem.at[i], recv_sem=pr_sem.at[i],
             device_id=dev, device_id_type=MESH)
 
-    src = (u, pk)
-    outs = (ua, pka)
-    for k in (1, 0):
-        for i in (2, 0, 1):
-            pair(k, src[k], me, (others[i], cx), s_sem, r_sem, i).start()
-        pair(k, src[k], me, (cy, 1 - cx), fs_sem, fr_sem, 3).start()
+    def rows(k):
+        return pl.ds(k * half, half)
+
+    def part(src, slot, k, dev, ss, rs, i):
+        return pltpu.make_async_remote_copy(
+            src_ref=src, dst_ref=ua.at[slot, rows(k)], send_sem=ss.at[i, k], recv_sem=rs.at[i, k],
+            device_id=dev, device_id_type=MESH)
+
+    partner = (cy, 1 - cx)
+    for i in range(3):
+        table(pk, me, (others[i], cx), i).start()
+    table(pk, me, partner, 3).start()
+    direct = [(1, 0), (0, 1), (1, 1), (0, 0)]
+    for i, k in direct:
+        part(u.at[rows(k)], me, k, (others[i], cx), s_sem, r_sem, i).start()
+    for k in range(2):
+        part(u.at[rows(k)], me, k, partner, os_sem, or_sem, 0).start()
     ua[me] = u[...]
     pka[me] = pk[...]
 
-    for c in shared:
-        c.wait()
-    for c in range(f // 256):
-        s = slice(c * 256, (c + 1) * 256)
-        z1 = jnp.dot(u[...], v1[:, s], preferred_element_type=F32)
-        z3 = jnp.dot(u[...], v3[:, s], preferred_element_type=F32)
-        gt[:, s] = _silu_mul(z1, z3)
-    for c in range(d // 512):
-        s = slice(c * 512, (c + 1) * 512)
-        hs[:, s] = h[:, s].astype(F32) + jnp.dot(gt[...], v2[:, s], preferred_element_type=F32)
-
-    def relay(k):
-        for i in (0, 1, 2):
-            slot = 2 * others[i] + cx
-            pair(k, src[k], slot, (others[i], cx), s_sem, r_sem, i).wait_recv()
-            pair(k, outs[k].at[slot], slot, (cy, 1 - cx), fs_sem, fr_sem, i).start()
-
-    def settle(k):
-        for i in (0, 1, 2):
-            slot = 2 * others[i] + cx
-            pair(k, outs[k].at[slot], slot, (cy, 1 - cx), fs_sem, fr_sem, i).wait()
-            pair(k, src[k], me, (others[i], cx), s_sem, r_sem, i).wait_send()
-        pair(k, src[k], me, (cy, 1 - cx), fs_sem, fr_sem, 3).wait()
-
-    relay(1)
-    settle(1)
-
-    tmap[...] = jnp.transpose(pka[...].reshape(ntok, 128))
-    ids = (me * ne + lax.broadcasted_iota(jnp.int32, (ne, ntok), 0)).astype(F32)
-    member = jnp.zeros((ne, ntok), F32)
-    gate = jnp.zeros((ne, ntok), F32)
-    for j in range(top):
-        hit = tmap[j:j + 1, :] == ids
-        member = member + jnp.where(hit, 1.0, 0.0)
-        gate = gate + jnp.where(hit, tmap[top + j:top + j + 1, :], 0.0)
-    ti = lax.broadcasted_iota(jnp.int32, (ntok, ntok), 0)
-    tj = lax.broadcasted_iota(jnp.int32, (ntok, ntok), 1)
-    tri = ti < tj
-    tri_b = (tri & (ti // blk == tj // blk)).astype(F32).astype(BF16)
-    rank = jnp.dot(member.astype(BF16), tri_b, preferred_element_type=F32)
-    keep = jnp.where(rank < cap, member, 0.0)
-    pos = jnp.dot(keep.astype(BF16), tri.astype(F32).astype(BF16), preferred_element_type=F32)
-    pkeep = jnp.where(keep > 0, pos, -1.0)
-    posk[...] = pkeep
-    both = jnp.concatenate([pkeep, gate * keep, jnp.zeros((128 - 2 * ne, ntok), F32)], axis=0)
-    cols[...] = jnp.transpose(both)
-
-    relay(0)
-    settle(0)
+    for i in range(3):
+        slot = 2 * others[i] + cx
+        table(pk, slot, (others[i], cx), i).wait_recv()
+        table(pka.at[slot], slot, partner, 4 + i).start()
+    for i in range(3):
+        slot = 2 * others[i] + cx
+        table(pka.at[slot], slot, partner, 4 + i).wait()
+        table(pk, me, (others[i], cx), i).wait_send()
+    table(pk, me, partner, 3).wait()
+
+    def tables():
+        tmap[...] = jnp.concatenate([pka[k, :, 0:blk] for k in range(8)], axis=1)
+        ids = (me * ne + lax.broadcasted_iota(jnp.int32, (ne, ntok), 0)).astype(F32)
+        member = jnp.zeros((ne, ntok), F32)
+        gate = jnp.zeros((ne, ntok), F32)
+        for j in range(top):
+            hit = tmap[j:j + 1, :] == ids
+            member = member + jnp.where(hit, 1.0, 0.0)
+            gate = gate + jnp.where(hit, tmap[top + j:top + j + 1, :], 0.0)
+        ti = lax.broadcasted_iota(jnp.int32, (ntok, ntok), 0)
+        tj = lax.broadcasted_iota(jnp.int32, (ntok, ntok), 1)
+        tri = ti < tj
+        tri_b = (tri & (ti // blk == tj // blk)).astype(F32).astype(BF16)
+        rank = jnp.dot(member.astype(BF16), tri_b, preferred_element_type=F32)
+        keep = jnp.where(rank < cap, member, 0.0)
+        pos = jnp.dot(keep.astype(BF16), tri.astype(F32).astype(BF16), preferred_element_type=F32)
+        pkeep = jnp.where(keep > 0, pos, -1.0)
+        posk[...] = pkeep
+        both = jnp.concatenate([pkeep, gate * keep, jnp.zeros((128 - 2 * ne, ntok), F32)], axis=0)
+        cols[...] = jnp.transpose(both)
+
+    def take(slot, k, dev, i):
+        part(u.at[rows(k)], slot, k, dev, s_sem, r_sem, i).wait_recv()
+        part(ua.at[slot, rows(k)], slot, k, partner, fs_sem, fr_sem, i).start()
+
+    sx, sy, sd = 2 * xn + cx, 2 * yn + cx, 2 * dg + cx
+    relay = {0: (sy, xn), 1: (sx, yn)}
+
+    def across(k):
+        slot, dev = relay[k]
+        return part(ua.at[slot, rows(k)], slot, k, (dev, cx), s_sem, r_sem, 2)
+
+    tables()
+    take(sy, 0, (yn, cx), 1)
+    across(0).start()
+    take(sx, 1, (xn, cx), 0)
+    across(1).start()
+    take(sy, 1, (yn, cx), 1)
+    take(sx, 0, (xn, cx), 0)
+    for k in range(2):
+        take(sd, k, (dg, cx), 2)
+    for i, slot in ((1, sy), (0, sx), (2, sd)):
+        for k in range(2):
+            part(ua.at[slot, rows(k)], slot, k, partner, fs_sem, fr_sem, i).wait()
+    for k in range(2):
+        part(u.at[rows(k)], me, k, partner, os_sem, or_sem, 0).wait()
+        across(k).wait_send()
+        for i in range(2):
+            part(u.at[rows(k)], me, k, (others[i], cx), s_sem, r_sem, i).wait_send()
     for cs in ahead:
         for c in cs:
             c.wait()
 
 
-def _all_gather(u, pk, h, ws1, ws3, ws2, w1, w3, w2):
+def _all_gather(u, pk, w1, w3, w2):
     b, d = u.shape
     ne, _, f = w1.shape
     return pl.pallas_call(
@@ -330,32 +348,30 @@
         out_shape=(pltpu.VMEM((8, b, d), BF16),
                    pltpu.VMEM((ne, 8 * b), F32),
                    pltpu.VMEM((8 * b, 128), F32),
-                   pltpu.VMEM((b, d), F32),
                    pltpu.VMEM((WBUF, d, f), BF16),
                    pltpu.VMEM((WBUF, d, f), BF16),
                    pltpu.VMEM((WBUF, f, d), BF16)),
-        in_specs=[_vm(), _vm(), _vm()] + [_any()] * 6,
-        out_specs=(_vm(),) * 7,
+        in_specs=[_vm(), _vm()] + [_hbm()] * 3,
+        out_specs=(_vm(),) * 6,
         scratch_shapes=[
-            pltpu.VMEM((8, b, 128), F32),
-            pltpu.VMEM((d, f), BF16),
-            pltpu.VMEM((d, f), BF16),
-            pltpu.VMEM((f, d), BF16),
-            pltpu.VMEM((b, f), BF16),
-            pltpu.VMEM((128, 8 * b), F32),
-            pltpu.SemaphoreType.DMA((2, 3)),
-            pltpu.SemaphoreType.DMA((2, 3)),
-            pltpu.SemaphoreType.DMA((2, 4)),
-            pltpu.SemaphoreType.DMA((2, 4)),
+            pltpu.VMEM((8, pk.shape[0], 128), F32),
+            pltpu.VMEM((pk.shape[0], 8 * b), F32),
+            pltpu.SemaphoreType.DMA((7,)),
+            pltpu.SemaphoreType.DMA((7,)),
+            pltpu.SemaphoreType.DMA((3, 2)),
+            pltpu.SemaphoreType.DMA((3, 2)),
+            pltpu.SemaphoreType.DMA((3, 2)),
+            pltpu.SemaphoreType.DMA((3, 2)),
+            pltpu.SemaphoreType.DMA((1, 2)),
+            pltpu.SemaphoreType.DMA((1, 2)),
             pltpu.SemaphoreType.DMA((3, WBUF)),
-            pltpu.SemaphoreType.DMA((3,)),
         ],
         compiler_params=pltpu.CompilerParams(
-            collective_id=0, has_side_effects=True, vmem_limit_bytes=12 * 1024 * 1024),
-    )(u, pk, h, ws1, ws3, ws2, w1, w3, w2)
-
-
-def _expert_kernel(ua, posk, cols, i1, i3, i2, w1, w3, w2, acc, b1, b3, b2, xt, gt, rt, psc, gsc, cnt, sem):
+            collective_id=0, has_side_effects=True, vmem_limit_bytes=4 * 1024 * 1024),
+    )(u, pk, w1, w3, w2)
+
+
+def _expert_kernel(ua, posk, cols, i1, i3, i2, w1, w3, w2, acc, b1, b3, b2, xt, gt, rt, psc, gsc, cnt, order, sem):
     del i1, i3, i2
     ntok, d = ua.shape
     ne = w1.shape[0]
@@ -368,6 +384,16 @@
 
     for e in range(ne):
         cnt[e] = (jnp.max(posk[e:e + 1, :]) + 1.0).astype(jnp.int32)
+    for e in range(ne):
+        if e < WBUF:
+            order[e] = e
+        else:
+            place = jnp.int32(WBUF)
+            for o in range(WBUF, ne):
+                if o != e:
+                    ahead = cnt[o] >= cnt[e] if o < e else cnt[o] > cnt[e]
+                    place = place + ahead.astype(jnp.int32)
+            order[place] = e
 
     def zero(i, _):
         acc[pl.ds(pl.multiple_of(i * 64, 64), 64), :] = jnp.zeros((64, d), F32)
@@ -384,10 +410,11 @@
             s = slice(c * dc, (c + 1) * dc)
             rt[:, s] = jnp.dot(gt[...], b2[slot, :, s], preferred_element_type=F32).astype(BF16)
 
-    def expert(e, _):
-        slot = lax.rem(e, WBUF)
-
-        @pl.when(e >= WBUF)
+    def expert(step, _):
+        slot = lax.rem(step, WBUF)
+        e = order[step]
+
+        @pl.when(step >= WBUF)
         def _():
             for c in copies(e, slot):
                 c.wait()
@@ -430,9 +457,9 @@
         lax.fori_loop(0, jnp.where(many, 0, (n + TILE - 1) // TILE), packed, 0)
         lax.fori_loop(0, jnp.where(many, ntok // TILE, 0), dense, 0)
 
-        @pl.when(e + WBUF < ne)
+        @pl.when(step + WBUF < ne)
         def _():
-            for c in copies(e + WBUF, slot):
+            for c in copies(order[step + WBUF], slot):
                 c.start()
         return 0
 
@@ -449,7 +476,7 @@
                    pltpu.VMEM((WBUF, d, f), BF16),
                    pltpu.VMEM((WBUF, d, f), BF16),
                    pltpu.VMEM((WBUF, f, d), BF16)),
-        in_specs=[_vm()] * 6 + [_any()] * 3,
+        in_specs=[_vm()] * 6 + [_hbm()] * 3,
         out_specs=(_vm(),) * 4,
         input_output_aliases={3: 1, 4: 2, 5: 3},
         scratch_shapes=[
@@ -459,33 +486,49 @@
             pltpu.VMEM((ntok, 128), F32),
             pltpu.VMEM((ntok, 128), F32),
             pltpu.SMEM((ne,), jnp.int32),
+            pltpu.SMEM((ne,), jnp.int32),
             pltpu.SemaphoreType.DMA((3, WBUF)),
         ],
-        compiler_params=pltpu.CompilerParams(vmem_limit_bytes=3584 * 1024),
+        compiler_params=pltpu.CompilerParams(vmem_limit_bytes=6144 * 1024),
     )(ua, posk, cols, i1, i3, i2, w1, w3, w2)[0]
 
 
 CH = 4
 
 
-def _return_kernel(acc, hs, y, rbuf, sbuf, gbuf, ds_sem, dr_sem, s_sem, r_sem):
+def _return_kernel(acc, h, u, ws1, ws3, ws2, y, rbuf, sbuf, abuf, tbuf, zbuf, hs, gt, v1, v3, v2,
+                   ds_sem, dr_sem, s_sem, r_sem, ts_sem, tr_sem, v_sem):
     cy, cx, others = _places()
+    xn, yn, dg = others
+    d = acc.shape[3]
+    f = gt.shape[1]
+    w = d // CH
+    n1 = xn * (1 - cx) + yn * cx
+    n2 = yn * (1 - cx) + xn * cx
+
+    shared = (pltpu.make_async_copy(ws1, v1, v_sem.at[0]),
+              pltpu.make_async_copy(ws3, v3, v_sem.at[1]),
+              pltpu.make_async_copy(ws2, v2, v_sem.at[2]))
+    for c in shared:
+        c.start()
     _barrier(cy, cx, others)
-    d = acc.shape[3]
-    w = d // CH
-
-    def cols(c):
-        return pl.ds(c * w, w)
 
     def pair(c):
         return pltpu.make_async_remote_copy(
-            src_ref=acc.at[:, 1 - cx, :, cols(c)], dst_ref=rbuf.at[c], send_sem=ds_sem.at[c], recv_sem=dr_sem.at[c],
+            src_ref=acc.at[:, 1 - cx, :, pl.ds(c * w, w)], dst_ref=rbuf.at[c],
+            send_sem=ds_sem.at[c], recv_sem=dr_sem.at[c],
             device_id=(cy, 1 - cx), device_id_type=MESH)
 
-    def far(c, i):
+    def first(c, i):
         return pltpu.make_async_remote_copy(
-            src_ref=sbuf.at[c, others[i]], dst_ref=gbuf.at[c, i], send_sem=s_sem.at[c, i], recv_sem=r_sem.at[c, i],
-            device_id=(others[i], cx), device_id_type=MESH)
+            src_ref=sbuf.at[c, dg if i else n1], dst_ref=abuf.at[c, i],
+            send_sem=s_sem.at[c, i], recv_sem=r_sem.at[c, i],
+            device_id=(n1, cx), device_id_type=MESH)
+
+    def second(c):
+        return pltpu.make_async_remote_copy(
+            src_ref=tbuf.at[c], dst_ref=zbuf.at[c], send_sem=ts_sem.at[c], recv_sem=tr_sem.at[c],
+            device_id=(n2, cx), device_id_type=MESH)
 
     for c in range(CH):
         pair(c).start()
@@ -493,51 +536,77 @@
         pair(c).wait_recv()
         for k in range(4):
             sbuf[c, k] = acc[k, cx, :, c * w:(c + 1) * w] + rbuf[c, k]
-        for i in (2, 0, 1):
-            far(c, i).start()
+        for i in (1, 0):
+            first(c, i).start()
+
+    for c in shared:
+        c.wait()
+    for c in range(f // 256):
+        s = slice(c * 256, (c + 1) * 256)
+        z1 = jnp.dot(u[...], v1[:, s], preferred_element_type=F32)
+        z3 = jnp.dot(u[...], v3[:, s], preferred_element_type=F32)
+        gt[:, s] = _silu_mul(z1, z3)
+    for c in range(d // 512):
+        s = slice(c * 512, (c + 1) * 512)
+        hs[:, s] = h[:, s].astype(F32) + jnp.dot(gt[...], v2[:, s], preferred_element_type=F32)
+
     for c in range(CH):
-        for i in range(3):
-            far(c, i).wait_recv()
+        first(c, 1).wait_recv()
+        tbuf[c] = sbuf[c, n2] + abuf[c, 1]
+        second(c).start()
+    for c in range(CH):
+        first(c, 0).wait_recv()
+        second(c).wait_recv()
         s = slice(c * w, (c + 1) * w)
-        t = hs[:, s] + sbuf[c, cy]
-        t = t + (gbuf[c, 0] + gbuf[c, 1] + gbuf[c, 2])
-        y[:, s] = t.astype(BF16)
+        y[:, s] = (hs[:, s] + sbuf[c, cy] + (abuf[c, 0] + zbuf[c])).astype(BF16)
     for c in range(CH):
         pair(c).wait_send()
-        for i in range(3):
-            far(c, i).wait_send()
-
-
-def _return(acc, hs):
-    b, d = hs.shape
+        for i in range(2):
+            first(c, i).wait_send()
+        second(c).wait_send()
+
+
+def _return(acc, h, u, ws1, ws3, ws2):
+    b, d = h.shape
+    f = ws1.shape[1]
     w = d // CH
     return pl.pallas_call(
         _return_kernel,
         name="giveback",
         out_shape=jax.ShapeDtypeStruct((b, d), BF16),
-        in_specs=[_vm(), _vm()],
+        in_specs=[_vm()] * 3 + [_hbm()] * 3,
         out_specs=_vm(),
         scratch_shapes=[
             pltpu.VMEM((CH, 4, b, w), F32),
             pltpu.VMEM((CH, 4, b, w), F32),
-            pltpu.VMEM((CH, 3, b, w), F32),
+            pltpu.VMEM((CH, 2, b, w), F32),
+            pltpu.VMEM((CH, b, w), F32),
+            pltpu.VMEM((CH, b, w), F32),
+            pltpu.VMEM((b, d), F32),
+            pltpu.VMEM((b, f), BF16),
+            pltpu.VMEM((d, f), BF16),
+            pltpu.VMEM((d, f), BF16),
+            pltpu.VMEM((f, d), BF16),
             pltpu.SemaphoreType.DMA((CH,)),
             pltpu.SemaphoreType.DMA((CH,)),
-            pltpu.SemaphoreType.DMA((CH, 3)),
-            pltpu.SemaphoreType.DMA((CH, 3)),
+            pltpu.SemaphoreType.DMA((CH, 2)),
+            pltpu.SemaphoreType.DMA((CH, 2)),
+            pltpu.SemaphoreType.DMA((CH,)),
+            pltpu.SemaphoreType.DMA((CH,)),
+            pltpu.SemaphoreType.DMA((3,)),
         ],
         compiler_params=pltpu.CompilerParams(
-            collective_id=1, has_side_effects=True, vmem_limit_bytes=9 * 1024 * 1024),
-    )(acc, hs)
+            collective_id=1, has_side_effects=True, vmem_limit_bytes=20 * 1024 * 1024),
+    )(acc, h, u, ws1, ws3, ws2)
 
 
 def solution(mesh):
     def body(x, kv_k, kv_v, lens, idx, gates, ln1, wq, wo, ln2, ws1, ws3, ws2, w1, w3, w2):
         b, d = x.shape
         h, u, pk = _attention(x, kv_k, kv_v, lens, idx, gates, ln1, ln2, wq, wo)
-        ua, posk, cols, hs, b1, b3, b2 = _all_gather(u, pk, h, ws1, ws3, ws2, w1, w3, w2)
+        ua, posk, cols, b1, b3, b2 = _all_gather(u, pk, w1, w3, w2)
         acc = _experts(ua.reshape(8 * b, d), posk, cols, b1, b3, b2, w1, w3, w2)
-        return _return(acc.reshape(4, 2, b, d), hs)
+        return _return(acc.reshape(4, 2, b, d), h, u, ws1, ws3, ws2)
 
     rows = P(GRP)
     rep = P()

time: 119 us -> 113 us (0.950)
  Pallas kernels: 118 us -> 112 us
    pallas_call x1, Pallas kernels: 19.4 us -> 15 us  [_all_gather(): pl.pallas_call(_gather_kernel, name='gather', out_shape=(pltpu.VMEM((8, b...]
where the time goes in v3:
time: 113 us
  Pallas kernels  112 us (99%)
    pallas_call x1, Pallas kernels, _experts(): pl.pallas_call(_expert_kernel, name='experts', out_shape=(pltpu.VMEM((nto...  41.3 us
    pallas_call x1, Pallas kernels, _return(): pl.pallas_call(_return_kernel, name='giveback', out_shape=jax.ShapeDtypeS...  32.8 us
    pallas_call x1, Pallas kernels, _attention(): pl.pallas_call(_attn_kernel, name='attn', out_shape=(pltpu.VMEM((b, d), B...  23.3 us
    pallas_call x1, Pallas kernels, _all_gather(): pl.pallas_call(_gather_kernel, name='gather', out_shape=(pltpu.VMEM((8, b...  15 us

profile of v3, /device:TPU:0, one launch (start us, length us, event | category | flops | bytes accessed | tf_op | source)
XLA Modules:
  0.0 113.2 jit_solution(12317283309711291284)
XLA Ops:
  0.0 23.3 %attn.1 = (bf16[64,2048]{1,0:T(8,128)(2,1)S(1)}, bf16[64,2048]{1,0:T(8,128)(2,1)S(1)}, f32[16,128]{1,0:T(8,128)S(1)}) custom-call(s32[64]{0:T(128)} %lens.1, bf16[64,2048]{1,0:T(8,128)(2,1)} %x.1, bf16[2048]{0:T(1024)(128)(2,1)} %ln1.1, bf16[2048]{0:T(1024)(128)(2,1)} %ln2.1, s32[8,64]{1,0:T(8,128)} %bitcast.10, f32[8,64]{1,0:T(8,128)} %bitcast.11, ...), custom_call_target="tpu_custom_call" | custom-call | tf_op jit(solution)/shard_map/attn/pallas_call | solution.py:176
  23.3 15.0 %gather.1 = (bf16[8,64,2048]{2,1,0:T(8,128)(2,1)S(1)}, f32[16,512]{1,0:T(8,128)S(1)}, f32[512,128]{1,0:T(8,128)S(1)}, bf16[4,2048,768]{2,1,0:T(8,128)(2,1)S(1)},...) custom-call(bf16[64,2048]{1,0:T(8,128)(2,1)S(1)} %get-tuple-element.15.u, ...), custom_call_target="tpu_custom_call" | custom-call | tf_op jit(solution)/shard_map/gather/pallas_call | solution.py:345
  38.3 0.0 copy-start
  38.3 0.0 copy-start.1
  38.3 0.0 copy-start.2
  38.3 41.3 %experts.1 = (f32[512,2048]{1,0:T(8,128)S(1)}, bf16[4,2048,768]{2,1,0:T(8,128)(2,1)S(1)}, bf16[4,2048,768]{2,1,0:T(8,128)(2,1)S(1)}, bf16[4,768,2048]{2,1,0:T(8,128)(2,1)S(1)}) custom-call(bf16[512,2048]{1,0:T(8,128)(2,1)S(1)} %bitcast.7, f32[16,512]{1,0:T(8,128)S(1)} %get-tuple-element.18.posk, ...), custom_call_target="tpu_custom_call", output_to_operand_aliasing={{1}: (3, {}), {2}: (4, {}), {3}: (5, {})} | custom-call | tf_op jit(solution)/shard_map/experts/pallas_call | solution.py:472
  79.6 0.0 copy-done
  79.6 0.0 copy-done.1
  79.7 0.0 copy-done.2
  79.7 32.8 %giveback.1 = bf16[64,2048]{1,0:T(8,128)(2,1)S(1)} custom-call(f32[4,2,64,2048]{3,2,1,0:T(8,128)S(1)} %bitcast.6, bf16[64,2048]{1,0:T(8,128)(2,1)S(1)} %get-tuple-element.24.h, bf16[64,2048]{1,0:T(8,128)(2,1)S(1)} %get-tuple-element.15.u, bf16[2048,768]{1,0:T(8,128)(2,1)S(1)} %copy-done, bf16[2048,768]{1,0:T(8,128)(2,1)S(1)} %copy-done.1, ...), custom_call_target="tpu_custom_call" | custom-call | tf_op jit(solution)/shard_map/giveback/pallas_call | solution.py:573
  112.5 0.7 copy.24
Async XLA Ops:
  38.3 41.4 %copy-start = (bf16[2048,768]{1,0:T(8,128)(2,1)S(1)}, bf16[2048,768]{1,0:T(8,128)(2,1)}, u32[]{:S(2)}) copy-start(bf16[2048,768]{1,0:T(8,128)(2,1)} %ws1.1) | copy-start | bytes 9437188
  38.3 41.3 %copy-start.1 = (bf16[2048,768]{1,0:T(8,128)(2,1)S(1)}, bf16[2048,768]{1,0:T(8,128)(2,1)}, u32[]{:S(2)}) copy-start(bf16[2048,768]{1,0:T(8,128)(2,1)} %ws3.1) | copy-start | bytes 9437188
  38.3 41.3 %copy-start.2 = (bf16[768,2048]{1,0:T(8,128)(2,1)S(1)}, bf16[768,2048]{1,0:T(8,128)(2,1)}, u32[]{:S(2)}) copy-start(bf16[768,2048]{1,0:T(8,128)(2,1)} %ws2.1) | copy-start | bytes 9437188

commit v4 on v3

--- a/solution.py
+++ b/solution.py
@@ -219,6 +219,9 @@
 
 WBUF = 4
 TILE = 128
+SMALL = 64
+LANES = 16
+STEP8 = 8
 
 
 def _silu_mul(z1, z3):
@@ -231,7 +234,7 @@
             pltpu.make_async_copy(w2.at[e], b2.at[slot], sem.at[2, slot]))
 
 
-def _gather_kernel(u, pk, w1, w3, w2, ua, posk, cols, b1, b3, b2,
+def _gather_kernel(u, pk, w1, w3, w2, ua, toks, wgts, cols, b1, b3, b2,
                    pka, tmap, ps_sem, pr_sem, s_sem, r_sem, fs_sem, fr_sem, os_sem, or_sem, w_sem):
     blk, d = u.shape
     ntok = 8 * blk
@@ -302,9 +305,23 @@
         keep = jnp.where(rank < cap, member, 0.0)
         pos = jnp.dot(keep.astype(BF16), tri.astype(F32).astype(BF16), preferred_element_type=F32)
         pkeep = jnp.where(keep > 0, pos, -1.0)
-        posk[...] = pkeep
-        both = jnp.concatenate([pkeep, gate * keep, jnp.zeros((128 - 2 * ne, ntok), F32)], axis=0)
+        gkeep = gate * keep
+        both = jnp.concatenate([gkeep, jnp.zeros((128 - ne, ntok), F32)], axis=0)
         cols[...] = jnp.transpose(both)
+        place = lax.broadcasted_iota(jnp.int32, (SMALL, ntok), 0).astype(F32)
+        tok = lax.broadcasted_iota(jnp.int32, (SMALL, ntok), 1).astype(F32) - ntok
+        lane = lax.broadcasted_iota(jnp.int32, (SMALL, 128), 1)
+        lists = jnp.zeros((SMALL, 128), F32)
+        for e in range(ne):
+            hit = pkeep[e:e + 1, :] == place
+            t = jnp.sum(jnp.where(hit, tok, 0.0), axis=1, keepdims=True)
+            g = jnp.sum(jnp.where(hit, gkeep[e:e + 1, :], 0.0), axis=1, keepdims=True)
+            lists = lists + jnp.where(lane == e, t, 0.0) + jnp.where(lane == ne + e, g, 0.0)
+        lists = jnp.transpose(jnp.concatenate([lists, jnp.zeros((128 - SMALL, 128), F32)], axis=0))
+        count = jnp.sum(keep, axis=1, keepdims=True)
+        last = lax.broadcasted_iota(jnp.int32, (ne, 128), 1) == 127
+        toks[...] = jnp.where(last, count, lists[0:ne, :] + ntok).astype(jnp.int32)
+        wgts[...] = lists[ne:2 * ne, :]
 
     def take(slot, k, dev, i):
         part(u.at[rows(k)], slot, k, dev, s_sem, r_sem, i).wait_recv()
@@ -346,13 +363,14 @@
         _gather_kernel,
         name="gather",
         out_shape=(pltpu.VMEM((8, b, d), BF16),
-                   pltpu.VMEM((ne, 8 * b), F32),
+                   jax.ShapeDtypeStruct((ne, 128), jnp.int32),
+                   jax.ShapeDtypeStruct((ne, 128), F32),
                    pltpu.VMEM((8 * b, 128), F32),
                    pltpu.VMEM((WBUF, d, f), BF16),
                    pltpu.VMEM((WBUF, d, f), BF16),
                    pltpu.VMEM((WBUF, f, d), BF16)),
         in_specs=[_vm(), _vm()] + [_hbm()] * 3,
-        out_specs=(_vm(),) * 6,
+        out_specs=(_vm(),) * 7,
         scratch_shapes=[
             pltpu.VMEM((8, pk.shape[0], 128), F32),
             pltpu.VMEM((pk.shape[0], 8 * b), F32),
@@ -371,7 +389,8 @@
     )(u, pk, w1, w3, w2)
 
 
-def _expert_kernel(ua, posk, cols, i1, i3, i2, w1, w3, w2, acc, b1, b3, b2, xt, gt, rt, psc, gsc, cnt, order, sem):
+def _expert_kernel(toks, wgts, ua, cols, i1, i3, i2, w1, w3, w2, acc, b1, b3, b2,
+                   ua3, x3, r3, xt, gt, rt, gsc, order, sem):
     del i1, i3, i2
     ntok, d = ua.shape
     ne = w1.shape[0]
@@ -382,8 +401,6 @@
     def copies(e, slot):
         return _slot_copies(w1, w3, w2, b1, b3, b2, sem, e, slot)
 
-    for e in range(ne):
-        cnt[e] = (jnp.max(posk[e:e + 1, :]) + 1.0).astype(jnp.int32)
     for e in range(ne):
         if e < WBUF:
             order[e] = e
@@ -391,24 +408,32 @@
             place = jnp.int32(WBUF)
             for o in range(WBUF, ne):
                 if o != e:
-                    ahead = cnt[o] >= cnt[e] if o < e else cnt[o] > cnt[e]
+                    ahead = toks[o, 127] >= toks[e, 127] if o < e else toks[o, 127] > toks[e, 127]
                     place = place + ahead.astype(jnp.int32)
             order[place] = e
 
+    for c in range(LANES):
+        ua3[pl.ds(c, ntok, stride=LANES), :] = ua[:, c * 128:(c + 1) * 128].astype(F32)
+    ua3[ntok * LANES:, :] = jnp.zeros((STEP8 * LANES, 128), F32)
+
     def zero(i, _):
-        acc[pl.ds(pl.multiple_of(i * 64, 64), 64), :] = jnp.zeros((64, d), F32)
+        acc[pl.ds(pl.multiple_of(i * 256, 256), 256), :] = jnp.zeros((256, 128), F32)
         return 0
-    lax.fori_loop(0, ntok // 64, zero, 0)
-
-    def ffn(slot):
+    lax.fori_loop(0, ntok * LANES // 256, zero, 0)
+    acc[ntok * LANES:, :] = jnp.zeros((STEP8 * LANES, 128), F32)
+
+    def hidden(slot, m):
         for c in range(f // fc):
             s = slice(c * fc, (c + 1) * fc)
-            z1 = jnp.dot(xt[...], b1[slot, :, s], preferred_element_type=F32)
-            z3 = jnp.dot(xt[...], b3[slot, :, s], preferred_element_type=F32)
-            gt[:, s] = _silu_mul(z1, z3)
-        for c in range(d // dc):
-            s = slice(c * dc, (c + 1) * dc)
-            rt[:, s] = jnp.dot(gt[...], b2[slot, :, s], preferred_element_type=F32).astype(BF16)
+            z1 = jnp.dot(xt[0:m, :], b1[slot, :, s], preferred_element_type=F32)
+            z3 = jnp.dot(xt[0:m, :], b3[slot, :, s], preferred_element_type=F32)
+            gt[0:m, s] = _silu_mul(z1, z3)
+
+    def result(slot, m, c):
+        return jnp.dot(gt[0:m, :], b2[slot, :, c * dc:(c + 1) * dc], preferred_element_type=F32).astype(BF16)
+
+    def at(t):
+        return pl.ds(pl.multiple_of(t * LANES, LANES), LANES)
 
     def expert(step, _):
         slot = lax.rem(step, WBUF)
@@ -418,44 +443,52 @@
         def _():
             for c in copies(e, slot):
                 c.wait()
-        n = cnt[e]
-        lane = lax.broadcasted_iota(jnp.int32, (ntok, 128), 1)
-        psc[...] = jnp.broadcast_to(
-            jnp.sum(jnp.where(lane == e, cols[...], 0.0), axis=1, keepdims=True), (ntok, 128))
-        gsc[...] = jnp.broadcast_to(
-            jnp.sum(jnp.where(lane == e + ne, cols[...], 0.0), axis=1, keepdims=True), (ntok, 128))
-
-        def packed(t, _):
-            base = t * TILE
-            want = (lax.broadcasted_iota(jnp.int32, (TILE, ntok), 0) + base).astype(F32)
-            sel = (posk[pl.ds(e, 1), :] == want).astype(F32).astype(BF16)
+        n = toks[e, 127]
+
+        @pl.when((n > 0) & (n <= SMALL))
+        def _():
+            steps = (n + STEP8 - 1) // STEP8
+
+            def fetch(i, _):
+                for k in range(STEP8):
+                    m = i * STEP8 + k
+                    x3[at(m), :] = ua3[at(toks[e, m]), :]
+                return 0
+            lax.fori_loop(0, steps, fetch, 0)
+            for c in range(LANES):
+                xt[0:SMALL, c * 128:(c + 1) * 128] = x3[pl.ds(c, SMALL, stride=LANES), :].astype(BF16)
+            hidden(slot, SMALL)
             for c in range(d // dc):
-                s = slice(c * dc, (c + 1) * dc)
-                xt[:, s] = jnp.dot(sel, ua[:, s], preferred_element_type=F32).astype(BF16)
-            ffn(slot)
-            wantc = (lax.broadcasted_iota(jnp.int32, (ntok, TILE), 1) + base).astype(F32)
-            selt = (psc[...] == wantc).astype(F32).astype(BF16)
-            for c in range(d // 256):
-                s = slice(c * 256, (c + 1) * 256)
-                y = jnp.dot(selt, rt[:, s], preferred_element_type=F32)
-                g = gsc[...]
-                acc[:, c * 256:c * 256 + 128] += g * y[:, 0:128]
-                acc[:, c * 256 + 128:(c + 1) * 256] += g * y[:, 128:256]
-            return 0
-
-        def dense(t, _):
-            rows = pl.ds(pl.multiple_of(t * TILE, TILE), TILE)
-            xt[...] = ua[rows, :]
-            ffn(slot)
-            g = gsc[rows, :]
-            for c in range(d // 128):
-                s = slice(c * 128, (c + 1) * 128)
-                acc[rows, s] += g * rt[:, s].astype(F32)
-            return 0
-
-        many = n > 2 * TILE
-        lax.fori_loop(0, jnp.where(many, 0, (n + TILE - 1) // TILE), packed, 0)
-        lax.fori_loop(0, jnp.where(many, ntok // TILE, 0), dense, 0)
+                y = result(slot, SMALL, c).astype(F32)
+                for j in range(dc // 128):
+                    r3[pl.ds(c * (dc // 128) + j, SMALL, stride=LANES), :] = y[:, j * 128:(j + 1) * 128]
+
+            def add(i, _):
+                where = [at(toks[e, i * STEP8 + k]) for k in range(STEP8)]
+                new = [acc[where[k], :] + wgts[e, i * STEP8 + k] * r3[at(i * STEP8 + k), :] for k in range(STEP8)]
+                for k in range(STEP8):
+                    acc[where[k], :] = new[k]
+                return 0
+            lax.fori_loop(0, steps, add, 0)
+
+        @pl.when(n > SMALL)
+        def _():
+            lane = lax.broadcasted_iota(jnp.int32, (ntok, 128), 1)
+            gsc[...] = jnp.broadcast_to(
+                jnp.sum(jnp.where(lane == e, cols[...], 0.0), axis=1, keepdims=True), (ntok, 128))
+
+            def dense(t, _):
+                rows = pl.ds(pl.multiple_of(t * TILE, TILE), TILE)
+                xt[...] = ua[rows, :]
+                hidden(slot, TILE)
+                for c in range(d // dc):
+                    rt[:, c * dc:(c + 1) * dc] = result(slot, TILE, c)
+                g = gsc[rows, :]
+                for c in range(LANES):
+                    where = pl.ds(t * (TILE * LANES) + c, TILE, stride=LANES)
+                    acc[where, :] = acc[where, :] + g * rt[:, c * 128:(c + 1) * 128].astype(F32)
+                return 0
+            lax.fori_loop(0, ntok // TILE, dense, 0)
 
         @pl.when(step + WBUF < ne)
         def _():
@@ -466,43 +499,45 @@
     lax.fori_loop(0, ne, expert, 0)
 
 
-def _experts(ua, posk, cols, i1, i3, i2, w1, w3, w2):
+def _experts(toks, wgts, ua, cols, i1, i3, i2, w1, w3, w2):
     ntok, d = ua.shape
     ne, _, f = w1.shape
     return pl.pallas_call(
         _expert_kernel,
         name="experts",
-        out_shape=(pltpu.VMEM((ntok, d), F32),
+        out_shape=(pltpu.VMEM(((ntok + STEP8) * LANES, 128), F32),
                    pltpu.VMEM((WBUF, d, f), BF16),
                    pltpu.VMEM((WBUF, d, f), BF16),
                    pltpu.VMEM((WBUF, f, d), BF16)),
-        in_specs=[_vm()] * 6 + [_hbm()] * 3,
+        in_specs=[_sm()] * 2 + [_vm()] * 5 + [_hbm()] * 3,
         out_specs=(_vm(),) * 4,
-        input_output_aliases={3: 1, 4: 2, 5: 3},
+        input_output_aliases={4: 1, 5: 2, 6: 3},
         scratch_shapes=[
+            pltpu.VMEM(((ntok + STEP8) * LANES, 128), F32),
+            pltpu.VMEM((SMALL * LANES, 128), F32),
+            pltpu.VMEM((SMALL * LANES, 128), F32),
             pltpu.VMEM((TILE, d), BF16),
             pltpu.VMEM((TILE, f), BF16),
             pltpu.VMEM((TILE, d), BF16),
             pltpu.VMEM((ntok, 128), F32),
-            pltpu.VMEM((ntok, 128), F32),
-            pltpu.SMEM((ne,), jnp.int32),
             pltpu.SMEM((ne,), jnp.int32),
             pltpu.SemaphoreType.DMA((3, WBUF)),
         ],
-        compiler_params=pltpu.CompilerParams(vmem_limit_bytes=6144 * 1024),
-    )(ua, posk, cols, i1, i3, i2, w1, w3, w2)[0]
+        compiler_params=pltpu.CompilerParams(vmem_limit_bytes=8 * 1024 * 1024),
+    )(toks, wgts, ua, cols, i1, i3, i2, w1, w3, w2)[0]
 
 
 CH = 4
 
 
-def _return_kernel(acc, h, u, ws1, ws3, ws2, y, rbuf, sbuf, abuf, tbuf, zbuf, hs, gt, v1, v3, v2,
+def _return_kernel(acc, h, u, ws1, ws3, ws2, y, rbuf, sbuf, abuf, tbuf, zbuf, tot, hs, gt, v1, v3, v2,
                    ds_sem, dr_sem, s_sem, r_sem, ts_sem, tr_sem, v_sem):
     cy, cx, others = _places()
     xn, yn, dg = others
-    d = acc.shape[3]
+    b, d = h.shape
     f = gt.shape[1]
-    w = d // CH
+    per = b // CH
+    w = per * LANES
     n1 = xn * (1 - cx) + yn * cx
     n2 = yn * (1 - cx) + xn * cx
 
@@ -513,10 +548,13 @@
         c.start()
     _barrier(cy, cx, others)
 
-    def pair(c):
+    def piece(k, core, c):
+        return pl.ds((2 * k + core) * (b * LANES) + c * w, w)
+
+    def pair(c, k):
         return pltpu.make_async_remote_copy(
-            src_ref=acc.at[:, 1 - cx, :, pl.ds(c * w, w)], dst_ref=rbuf.at[c],
-            send_sem=ds_sem.at[c], recv_sem=dr_sem.at[c],
+            src_ref=acc.at[piece(k, 1 - cx, c)], dst_ref=rbuf.at[c, k],
+            send_sem=ds_sem.at[c, k], recv_sem=dr_sem.at[c, k],
             device_id=(cy, 1 - cx), device_id_type=MESH)
 
     def first(c, i):
@@ -531,11 +569,12 @@
             device_id=(n2, cx), device_id_type=MESH)
 
     for c in range(CH):
-        pair(c).start()
+        for k in range(4):
+            pair(c, k).start()
     for c in range(CH):
-        pair(c).wait_recv()
         for k in range(4):
-            sbuf[c, k] = acc[k, cx, :, c * w:(c + 1) * w] + rbuf[c, k]
+            pair(c, k).wait_recv()
+            sbuf[c, k] = acc[piece(k, cx, c), :] + rbuf[c, k]
         for i in (1, 0):
             first(c, i).start()
 
@@ -557,10 +596,14 @@
     for c in range(CH):
         first(c, 0).wait_recv()
         second(c).wait_recv()
-        s = slice(c * w, (c + 1) * w)
-        y[:, s] = (hs[:, s] + sbuf[c, cy] + (abuf[c, 0] + zbuf[c])).astype(BF16)
+        tot[...] = sbuf[c, cy] + (abuf[c, 0] + zbuf[c])
+        r = slice(c * per, (c + 1) * per)
+        for j in range(LANES):
+            s = slice(j * 128, (j + 1) * 128)
+            y[r, s] = (hs[r, s] + tot[pl.ds(j, per, stride=LANES), :]).astype(BF16)
     for c in range(CH):
-        pair(c).wait_send()
+        for k in range(4):
+            pair(c, k).wait_send()
         for i in range(2):
             first(c, i).wait_send()
         second(c).wait_send()
@@ -569,7 +612,7 @@
 def _return(acc, h, u, ws1, ws3, ws2):
     b, d = h.shape
     f = ws1.shape[1]
-    w = d // CH
+    w = b // CH * LANES
     return pl.pallas_call(
         _return_kernel,
         name="giveback",
@@ -577,18 +620,19 @@
         in_specs=[_vm()] * 3 + [_hbm()] * 3,
         out_specs=_vm(),
         scratch_shapes=[
-            pltpu.VMEM((CH, 4, b, w), F32),
-            pltpu.VMEM((CH, 4, b, w), F32),
-            pltpu.VMEM((CH, 2, b, w), F32),
-            pltpu.VMEM((CH, b, w), F32),
-            pltpu.VMEM((CH, b, w), F32),
+            pltpu.VMEM((CH, 4, w, 128), F32),
+            pltpu.VMEM((CH, 4, w, 128), F32),
+            pltpu.VMEM((CH, 2, w, 128), F32),
+            pltpu.VMEM((CH, w, 128), F32),
+            pltpu.VMEM((CH, w, 128), F32),
+            pltpu.VMEM((w, 128), F32),
             pltpu.VMEM((b, d), F32),
             pltpu.VMEM((b, f), BF16),
             pltpu.VMEM((d, f), BF16),
             pltpu.VMEM((d, f), BF16),
             pltpu.VMEM((f, d), BF16),
-            pltpu.SemaphoreType.DMA((CH,)),
-            pltpu.SemaphoreType.DMA((CH,)),
+            pltpu.SemaphoreType.DMA((CH, 4)),
+            pltpu.SemaphoreType.DMA((CH, 4)),
             pltpu.SemaphoreType.DMA((CH, 2)),
             pltpu.SemaphoreType.DMA((CH, 2)),
             pltpu.SemaphoreType.DMA((CH,)),
@@ -604,9 +648,9 @@
     def body(x, kv_k, kv_v, lens, idx, gates, ln1, wq, wo, ln2, ws1, ws3, ws2, w1, w3, w2):
         b, d = x.shape
         h, u, pk = _attention(x, kv_k, kv_v, lens, idx, gates, ln1, ln2, wq, wo)
-        ua, posk, cols, b1, b3, b2 = _all_gather(u, pk, w1, w3, w2)
-        acc = _experts(ua.reshape(8 * b, d), posk, cols, b1, b3, b2, w1, w3, w2)
-        return _return(acc.reshape(4, 2, b, d), h, u, ws1, ws3, ws2)
+        ua, toks, wgts, cols, b1, b3, b2 = _all_gather(u, pk, w1, w3, w2)
+        acc = _experts(toks, wgts, ua.reshape(8 * b, d), cols, b1, b3, b2, w1, w3, w2)
+        return _return(acc, h, u, ws1, ws3, ws2)
 
     rows = P(GRP)
     rep = P()

time: 113 us -> 114 us (level)
  no operation moved by 1% of the time
where the time goes in v4:
time: 114 us
  Pallas kernels  113 us (99%)
    pallas_call x1, Pallas kernels, _experts(): pl.pallas_call(_expert_kernel, name='experts', out_shape=(pltpu.VMEM(((nt...  41.3 us
    pallas_call x1, Pallas kernels, _return(): pl.pallas_call(_return_kernel, name='giveback', out_shape=jax.ShapeDtypeS...  33.3 us
    pallas_call x1, Pallas kernels, _attention(): pl.pallas_call(_attn_kernel, name='attn', out_shape=(pltpu.VMEM((b, d), B...  23.3 us
    pallas_call x1, Pallas kernels, _all_gather(): pl.pallas_call(_gather_kernel, name='gather', out_shape=(pltpu.VMEM((8, b...  15.4 us

profile of v4, /device:TPU:0, one launch (start us, length us, event | category | flops | bytes accessed | tf_op | source)
XLA Modules:
  0.0 114.1 jit_solution(3510985557498770122)
XLA Ops:
  0.0 23.3 %attn.1 = (bf16[64,2048]{1,0:T(8,128)(2,1)S(1)}, bf16[64,2048]{1,0:T(8,128)(2,1)S(1)}, f32[16,128]{1,0:T(8,128)S(1)}) custom-call(s32[64]{0:T(128)} %lens.1, bf16[64,2048]{1,0:T(8,128)(2,1)} %x.1, bf16[2048]{0:T(1024)(128)(2,1)} %ln1.1, bf16[2048]{0:T(1024)(128)(2,1)} %ln2.1, s32[8,64]{1,0:T(8,128)} %bitcast.8, f32[8,64]{1,0:T(8,128)} %bitcast.9, ...), custom_call_target="tpu_custom_call" | custom-call | tf_op jit(solution)/shard_map/attn/pallas_call | solution.py:176
  23.3 15.4 %gather.1 = (bf16[8,64,2048]{2,1,0:T(8,128)(2,1)S(1)}, s32[16,128]{1,0:T(8,128)S(1)}, f32[16,128]{1,0:T(8,128)S(1)}, f32[512,128]{1,0:T(8,128)S(1)}, bf16[4,2048...) custom-call(bf16[64,2048]{1,0:T(8,128)(2,1)S(1)} %get-tuple-element.16.u, ...), custom_call_target="tpu_custom_call" | custom-call | tf_op jit(solution)/shard_map/gather/pallas_call | solution.py:362
  38.7 0.0 copy-start
  38.7 0.0 copy-start.1
  38.7 0.0 copy-start.2
  38.8 41.3 %experts.1 = (f32[8320,128]{1,0:T(8,128)S(1)}, bf16[4,2048,768]{2,1,0:T(8,128)(2,1)S(1)}, bf16[4,2048,768]{2,1,0:T(8,128)(2,1)S(1)}, bf16[4,768,2048]{2,1,0:T(8,128)(2,1)S(1)}) custom-call(s32[16,128]{1,0:T(8,128)S(1)} %get-tuple-element.18.toks, f32[16,128]{1,0:T(8,128)S(1)} %get-tuple-element.19.wgts, ...), custom_call_target="tpu_custom_call", output_to_operand_aliasing={{1}: (4, {}), {2}: (5, {}), {3}: (6, {})} | custom-call | tf_op jit(solution)/shard_map/experts/pallas_call | solution.py:505
  80.0 0.0 copy-done
  80.0 0.0 copy-done.1
  80.0 0.0 copy-done.2
  80.0 33.3 %giveback.1 = bf16[64,2048]{1,0:T(8,128)(2,1)S(1)} custom-call(f32[8320,128]{1,0:T(8,128)S(1)} %get-tuple-element.25.acc, bf16[64,2048]{1,0:T(8,128)(2,1)S(1)} %get-tuple-element.26.h, bf16[64,2048]{1,0:T(8,128)(2,1)S(1)} %get-tuple-element.16.u, bf16[2048,768]{1,0:T(8,128)(2,1)S(1)} %copy-done, bf16[2048,768]{1,0:T(8,128)(2,1)S(1)} %copy-done.1, ...), custom_call_target="tpu_custom_call" | custom-call | tf_op jit(solution)/shard_map/giveback/pallas_call | solution.py:616
  113.4 0.7 copy.24
Async XLA Ops:
  38.7 41.3 %copy-start = (bf16[2048,768]{1,0:T(8,128)(2,1)S(1)}, bf16[2048,768]{1,0:T(8,128)(2,1)}, u32[]{:S(2)}) copy-start(bf16[2048,768]{1,0:T(8,128)(2,1)} %ws1.1) | copy-start | bytes 9437188
  38.7 41.3 %copy-start.1 = (bf16[2048,768]{1,0:T(8,128)(2,1)S(1)}, bf16[2048,768]{1,0:T(8,128)(2,1)}, u32[]{:S(2)}) copy-start(bf16[2048,768]{1,0:T(8,128)(2,1)} %ws3.1) | copy-start | bytes 9437188
  38.7 41.3 %copy-start.2 = (bf16[768,2048]{1,0:T(8,128)(2,1)S(1)}, bf16[768,2048]{1,0:T(8,128)(2,1)}, u32[]{:S(2)}) copy-start(bf16[768,2048]{1,0:T(8,128)(2,1)} %ws2.1) | copy-start | bytes 9437188

commit v5 on v4

--- a/solution.py
+++ b/solution.py
@@ -390,7 +390,7 @@
 
 
 def _expert_kernel(toks, wgts, ua, cols, i1, i3, i2, w1, w3, w2, acc, b1, b3, b2,
-                   ua3, x3, r3, xt, gt, rt, gsc, order, sem):
+                   ua3, x3, r3, xt, gt, rt, gsc, order, seat, sem):
     del i1, i3, i2
     ntok, d = ua.shape
     ne = w1.shape[0]
@@ -401,16 +401,19 @@
     def copies(e, slot):
         return _slot_copies(w1, w3, w2, b1, b3, b2, sem, e, slot)
 
+    spread = [5, 9, 12, 7, 10, 4, 6, 8, 11, 13, 14, 15]
+    for k in range(ne - WBUF):
+        seat[k] = spread[k]
     for e in range(ne):
         if e < WBUF:
             order[e] = e
         else:
-            place = jnp.int32(WBUF)
+            rank = jnp.int32(0)
             for o in range(WBUF, ne):
                 if o != e:
                     ahead = toks[o, 127] >= toks[e, 127] if o < e else toks[o, 127] > toks[e, 127]
-                    place = place + ahead.astype(jnp.int32)
-            order[place] = e
+                    rank = rank + ahead.astype(jnp.int32)
+            order[seat[rank]] = e
 
     for c in range(LANES):
         ua3[pl.ds(c, ntok, stride=LANES), :] = ua[:, c * 128:(c + 1) * 128].astype(F32)
@@ -520,6 +523,7 @@
             pltpu.VMEM((TILE, f), BF16),
             pltpu.VMEM((TILE, d), BF16),
             pltpu.VMEM((ntok, 128), F32),
+            pltpu.SMEM((ne,), jnp.int32),
             pltpu.SMEM((ne,), jnp.int32),
             pltpu.SemaphoreType.DMA((3, WBUF)),
         ],

time: 114 us -> 112 us (0.982)
  Pallas kernels: 113 us -> 111 us
    pallas_call x1, Pallas kernels: 33.3 us -> 31.5 us  [_return(): pl.pallas_call(_return_kernel, name='giveback', out_shape=jax.ShapeDtypeS...]
where the time goes in v5:
time: 112 us
  Pallas kernels  111 us (99%)
    pallas_call x1, Pallas kernels, _experts(): pl.pallas_call(_expert_kernel, name='experts', out_shape=(pltpu.VMEM(((nt...  41.1 us
    pallas_call x1, Pallas kernels, _return(): pl.pallas_call(_return_kernel, name='giveback', out_shape=jax.ShapeDtypeS...  31.5 us
    pallas_call x1, Pallas kernels, _attention(): pl.pallas_call(_attn_kernel, name='attn', out_shape=(pltpu.VMEM((b, d), B...  23.3 us
    pallas_call x1, Pallas kernels, _all_gather(): pl.pallas_call(_gather_kernel, name='gather', out_shape=(pltpu.VMEM((8, b...  15.4 us

profile of v5, /device:TPU:0, one launch (start us, length us, event | category | flops | bytes accessed | tf_op | source)
XLA Modules:
  0.0 112.1 jit_solution(8429598190509852747)
XLA Ops:
  0.0 23.3 %attn.1 = (bf16[64,2048]{1,0:T(8,128)(2,1)S(1)}, bf16[64,2048]{1,0:T(8,128)(2,1)S(1)}, f32[16,128]{1,0:T(8,128)S(1)}) custom-call(s32[64]{0:T(128)} %lens.1, bf16[64,2048]{1,0:T(8,128)(2,1)} %x.1, bf16[2048]{0:T(1024)(128)(2,1)} %ln1.1, bf16[2048]{0:T(1024)(128)(2,1)} %ln2.1, s32[8,64]{1,0:T(8,128)} %bitcast.8, f32[8,64]{1,0:T(8,128)} %bitcast.9, ...), custom_call_target="tpu_custom_call" | custom-call | tf_op jit(solution)/shard_map/attn/pallas_call | solution.py:176
  23.3 15.4 %gather.1 = (bf16[8,64,2048]{2,1,0:T(8,128)(2,1)S(1)}, s32[16,128]{1,0:T(8,128)S(1)}, f32[16,128]{1,0:T(8,128)S(1)}, f32[512,128]{1,0:T(8,128)S(1)}, bf16[4,2048...) custom-call(bf16[64,2048]{1,0:T(8,128)(2,1)S(1)} %get-tuple-element.16.u, ...), custom_call_target="tpu_custom_call" | custom-call | tf_op jit(solution)/shard_map/gather/pallas_call | solution.py:362
  38.7 0.0 copy-start
  38.7 0.0 copy-start.1
  38.7 0.0 copy-start.2
  38.8 41.1 %experts.1 = (f32[8320,128]{1,0:T(8,128)S(1)}, bf16[4,2048,768]{2,1,0:T(8,128)(2,1)S(1)}, bf16[4,2048,768]{2,1,0:T(8,128)(2,1)S(1)}, bf16[4,768,2048]{2,1,0:T(8,128)(2,1)S(1)}) custom-call(s32[16,128]{1,0:T(8,128)S(1)} %get-tuple-element.18.toks, f32[16,128]{1,0:T(8,128)S(1)} %get-tuple-element.19.wgts, ...), custom_call_target="tpu_custom_call", output_to_operand_aliasing={{1}: (4, {}), {2}: (5, {}), {3}: (6, {})} | custom-call | tf_op jit(solution)/shard_map/experts/pallas_call | solution.py:508
  79.9 0.0 copy-done
  79.9 0.0 copy-done.1
  79.9 0.0 copy-done.2
  79.9 31.5 %giveback.1 = bf16[64,2048]{1,0:T(8,128)(2,1)S(1)} custom-call(f32[8320,128]{1,0:T(8,128)S(1)} %get-tuple-element.25.acc, bf16[64,2048]{1,0:T(8,128)(2,1)S(1)} %get-tuple-element.26.h, bf16[64,2048]{1,0:T(8,128)(2,1)S(1)} %get-tuple-element.16.u, bf16[2048,768]{1,0:T(8,128)(2,1)S(1)} %copy-done, bf16[2048,768]{1,0:T(8,128)(2,1)S(1)} %copy-done.1, ...), custom_call_target="tpu_custom_call" | custom-call | tf_op jit(solution)/shard_map/giveback/pallas_call | solution.py:620
  111.4 0.7 copy.24
Async XLA Ops:
  38.7 41.1 %copy-start = (bf16[2048,768]{1,0:T(8,128)(2,1)S(1)}, bf16[2048,768]{1,0:T(8,128)(2,1)}, u32[]{:S(2)}) copy-start(bf16[2048,768]{1,0:T(8,128)(2,1)} %ws1.1) | copy-start | bytes 9437188
  38.7 41.1 %copy-start.1 = (bf16[2048,768]{1,0:T(8,128)(2,1)S(1)}, bf16[2048,768]{1,0:T(8,128)(2,1)}, u32[]{:S(2)}) copy-start(bf16[2048,768]{1,0:T(8,128)(2,1)} %ws3.1) | copy-start | bytes 9437188
  38.7 41.1 %copy-start.2 = (bf16[768,2048]{1,0:T(8,128)(2,1)S(1)}, bf16[768,2048]{1,0:T(8,128)(2,1)}, u32[]{:S(2)}) copy-start(bf16[768,2048]{1,0:T(8,128)(2,1)} %ws2.1) | copy-start | bytes 9437188

commit v6 on v5

--- a/solution.py
+++ b/solution.py
@@ -221,6 +221,7 @@
 TILE = 128
 SMALL = 64
 LANES = 16
+PITCH = 17
 STEP8 = 8
 
 
@@ -389,9 +390,9 @@
     )(u, pk, w1, w3, w2)
 
 
-def _expert_kernel(toks, wgts, ua, cols, i1, i3, i2, w1, w3, w2, acc, b1, b3, b2,
-                   ua3, x3, r3, xt, gt, rt, gsc, order, seat, sem):
-    del i1, i3, i2
+def _expert_kernel(toks, wgts, ua, cols, b1, b3, b2, w1, w3, w2, acc, o1, o3, o2,
+                   ua3, x3, r3, xt, gt, gsc, order, seat, sem):
+    del o1, o3, o2
     ntok, d = ua.shape
     ne = w1.shape[0]
     f = w1.shape[2]
@@ -416,8 +417,8 @@
             order[seat[rank]] = e
 
     for c in range(LANES):
-        ua3[pl.ds(c, ntok, stride=LANES), :] = ua[:, c * 128:(c + 1) * 128].astype(F32)
-    ua3[ntok * LANES:, :] = jnp.zeros((STEP8 * LANES, 128), F32)
+        ua3[pl.ds(c, ntok, stride=PITCH), :] = ua[:, c * 128:(c + 1) * 128].astype(F32)
+    ua3[ntok * PITCH:, :] = jnp.zeros((STEP8 * PITCH, 128), F32)
 
     def zero(i, _):
         acc[pl.ds(pl.multiple_of(i * 256, 256), 256), :] = jnp.zeros((256, 128), F32)
@@ -432,11 +433,18 @@
             z3 = jnp.dot(xt[0:m, :], b3[slot, :, s], preferred_element_type=F32)
             gt[0:m, s] = _silu_mul(z1, z3)
 
-    def result(slot, m, c):
-        return jnp.dot(gt[0:m, :], b2[slot, :, c * dc:(c + 1) * dc], preferred_element_type=F32).astype(BF16)
+    def results(slot, m):
+        for c in range(d // dc):
+            y = jnp.dot(gt[0:m, :], b2[slot, :, c * dc:(c + 1) * dc], preferred_element_type=F32)
+            y = y.astype(BF16).astype(F32)
+            for j in range(dc // 128):
+                r3[pl.ds(c * (dc // 128) + j, m, stride=PITCH), :] = y[:, j * 128:(j + 1) * 128]
 
     def at(t):
         return pl.ds(pl.multiple_of(t * LANES, LANES), LANES)
+
+    def wide(t):
+        return pl.ds(t * PITCH, LANES)
 
     def expert(step, _):
         slot = lax.rem(step, WBUF)
@@ -455,20 +463,17 @@
             def fetch(i, _):
                 for k in range(STEP8):
                     m = i * STEP8 + k
-                    x3[at(m), :] = ua3[at(toks[e, m]), :]
+                    x3[wide(m), :] = ua3[wide(toks[e, m]), :]
                 return 0
             lax.fori_loop(0, steps, fetch, 0)
             for c in range(LANES):
-                xt[0:SMALL, c * 128:(c + 1) * 128] = x3[pl.ds(c, SMALL, stride=LANES), :].astype(BF16)
+                xt[0:SMALL, c * 128:(c + 1) * 128] = x3[pl.ds(c, SMALL, stride=PITCH), :].astype(BF16)
             hidden(slot, SMALL)
-            for c in range(d // dc):
-                y = result(slot, SMALL, c).astype(F32)
-                for j in range(dc // 128):
-                    r3[pl.ds(c * (dc // 128) + j, SMALL, stride=LANES), :] = y[:, j * 128:(j + 1) * 128]
+            results(slot, SMALL)
 
             def add(i, _):
                 where = [at(toks[e, i * STEP8 + k]) for k in range(STEP8)]
-                new = [acc[where[k], :] + wgts[e, i * STEP8 + k] * r3[at(i * STEP8 + k), :] for k in range(STEP8)]
+                new = [acc[where[k], :] + wgts[e, i * STEP8 + k] * r3[wide(i * STEP8 + k), :] for k in range(STEP8)]
                 for k in range(STEP8):
                     acc[where[k], :] = new[k]
                 return 0
@@ -484,12 +489,16 @@
                 rows = pl.ds(pl.multiple_of(t * TILE, TILE), TILE)
                 xt[...] = ua[rows, :]
                 hidden(slot, TILE)
-                for c in range(d // dc):
-                    rt[:, c * dc:(c + 1) * dc] = result(slot, TILE, c)
-                g = gsc[rows, :]
-                for c in range(LANES):
-                    where = pl.ds(t * (TILE * LANES) + c, TILE, stride=LANES)
-                    acc[where, :] = acc[where, :] + g * rt[:, c * 128:(c + 1) * 128].astype(F32)
+                results(slot, TILE)
+
+                def add(i, _):
+                    for k in range(STEP8):
+                        m = i * STEP8 + k
+                        one = at(t * TILE + m)
+                        g = gsc[pl.ds(t * TILE + m, 1), :]
+                        acc[one, :] = acc[one, :] + g * r3[wide(m), :]
+                    return 0
+                lax.fori_loop(0, TILE // STEP8, add, 0)
                 return 0
             lax.fori_loop(0, ntok // TILE, dense, 0)
 
@@ -516,18 +525,17 @@
         out_specs=(_vm(),) * 4,
         input_output_aliases={4: 1, 5: 2, 6: 3},
         scratch_shapes=[
-            pltpu.VMEM(((ntok + STEP8) * LANES, 128), F32),
-            pltpu.VMEM((SMALL * LANES, 128), F32),
-            pltpu.VMEM((SMALL * LANES, 128), F32),
+            pltpu.VMEM(((ntok + STEP8) * PITCH, 128), F32),
+            pltpu.VMEM((SMALL * PITCH, 128), F32),
+            pltpu.VMEM((TILE * PITCH, 128), F32),
             pltpu.VMEM((TILE, d), BF16),
             pltpu.VMEM((TILE, f), BF16),
-            pltpu.VMEM((TILE, d), BF16),
             pltpu.VMEM((ntok, 128), F32),
             pltpu.SMEM((ne,), jnp.int32),
             pltpu.SMEM((ne,), jnp.int32),
             pltpu.SemaphoreType.DMA((3, WBUF)),
         ],
-        compiler_params=pltpu.CompilerParams(vmem_limit_bytes=8 * 1024 * 1024),
+        compiler_params=pltpu.CompilerParams(vmem_limit_bytes=9 * 1024 * 1024),
     )(toks, wgts, ua, cols, i1, i3, i2, w1, w3, w2)[0]
 
 

time: 112 us -> 108 us (0.964)
  Pallas kernels: 111 us -> 108 us
    pallas_call x1, Pallas kernels: 41.1 us -> 39.2 us  [_experts(): pl.pallas_call(_expert_kernel, name='experts', out_shape=(pltpu.VMEM(((nt...]
    pallas_call x1, Pallas kernels: 31.5 us -> 29.8 us  [_return(): pl.pallas_call(_return_kernel, name='giveback', out_shape=jax.ShapeDtypeS...]
where the time goes in v6:
time: 108 us
  Pallas kernels  108 us (100%)
    pallas_call x1, Pallas kernels, _experts(): pl.pallas_call(_expert_kernel, name='experts', out_shape=(pltpu.VMEM(((nt...  39.2 us
    pallas_call x1, Pallas kernels, _return(): pl.pallas_call(_return_kernel, name='giveback', out_shape=jax.ShapeDtypeS...  29.8 us
    pallas_call x1, Pallas kernels, _attention(): pl.pallas_call(_attn_kernel, name='attn', out_shape=(pltpu.VMEM((b, d), B...  23.3 us
    pallas_call x1, Pallas kernels, _all_gather(): pl.pallas_call(_gather_kernel, name='gather', out_shape=(pltpu.VMEM((8, b...  15.4 us

profile of v6, /device:TPU:0, one launch (start us, length us, event | category | flops | bytes accessed | tf_op | source)
XLA Modules:
  0.0 108.5 jit_solution(11659425524232593618)
XLA Ops:
  0.0 23.3 %attn.1 = (bf16[64,2048]{1,0:T(8,128)(2,1)S(1)}, bf16[64,2048]{1,0:T(8,128)(2,1)S(1)}, f32[16,128]{1,0:T(8,128)S(1)}) custom-call(s32[64]{0:T(128)} %lens.1, bf16[64,2048]{1,0:T(8,128)(2,1)} %x.1, bf16[2048]{0:T(1024)(128)(2,1)} %ln1.1, bf16[2048]{0:T(1024)(128)(2,1)} %ln2.1, s32[8,64]{1,0:T(8,128)} %bitcast.8, f32[8,64]{1,0:T(8,128)} %bitcast.9, ...), custom_call_target="tpu_custom_call" | custom-call | tf_op jit(solution)/shard_map/attn/pallas_call | solution.py:176
  23.3 15.4 %gather.1 = (bf16[8,64,2048]{2,1,0:T(8,128)(2,1)S(1)}, s32[16,128]{1,0:T(8,128)S(1)}, f32[16,128]{1,0:T(8,128)S(1)}, f32[512,128]{1,0:T(8,128)S(1)}, bf16[4,2048...) custom-call(bf16[64,2048]{1,0:T(8,128)(2,1)S(1)} %get-tuple-element.16.u, ...), custom_call_target="tpu_custom_call" | custom-call | tf_op jit(solution)/shard_map/gather/pallas_call | solution.py:363
  38.7 0.0 copy-start
  38.7 0.0 copy-start.1
  38.7 0.0 copy-start.2
  38.8 39.2 %experts.1 = (f32[8320,128]{1,0:T(8,128)S(1)}, bf16[4,2048,768]{2,1,0:T(8,128)(2,1)S(1)}, bf16[4,2048,768]{2,1,0:T(8,128)(2,1)S(1)}, bf16[4,768,2048]{2,1,0:T(8,128)(2,1)S(1)}) custom-call(s32[16,128]{1,0:T(8,128)S(1)} %get-tuple-element.18.toks, f32[16,128]{1,0:T(8,128)S(1)} %get-tuple-element.19.wgts, ...), custom_call_target="tpu_custom_call", output_to_operand_aliasing={{1}: (4, {}), {2}: (5, {}), {3}: (6, {})} | custom-call | tf_op jit(solution)/shard_map/experts/pallas_call | solution.py:517
  78.0 0.0 copy-done
  78.0 0.0 copy-done.1
  78.0 0.0 copy-done.2
  78.0 29.8 %giveback.1 = bf16[64,2048]{1,0:T(8,128)(2,1)S(1)} custom-call(f32[8320,128]{1,0:T(8,128)S(1)} %get-tuple-element.25.acc, bf16[64,2048]{1,0:T(8,128)(2,1)S(1)} %get-tuple-element.26.h, bf16[64,2048]{1,0:T(8,128)(2,1)S(1)} %get-tuple-element.16.u, bf16[2048,768]{1,0:T(8,128)(2,1)S(1)} %copy-done, bf16[2048,768]{1,0:T(8,128)(2,1)S(1)} %copy-done.1, ...), custom_call_target="tpu_custom_call" | custom-call | tf_op jit(solution)/shard_map/giveback/pallas_call | solution.py:628
  107.8 0.7 copy.24
Async XLA Ops:
  38.7 39.3 %copy-start = (bf16[2048,768]{1,0:T(8,128)(2,1)S(1)}, bf16[2048,768]{1,0:T(8,128)(2,1)}, u32[]{:S(2)}) copy-start(bf16[2048,768]{1,0:T(8,128)(2,1)} %ws1.1) | copy-start | bytes 9437188
  38.7 39.3 %copy-start.1 = (bf16[2048,768]{1,0:T(8,128)(2,1)S(1)}, bf16[2048,768]{1,0:T(8,128)(2,1)}, u32[]{:S(2)}) copy-start(bf16[2048,768]{1,0:T(8,128)(2,1)} %ws3.1) | copy-start | bytes 9437188
  38.7 39.3 %copy-start.2 = (bf16[768,2048]{1,0:T(8,128)(2,1)S(1)}, bf16[768,2048]{1,0:T(8,128)(2,1)}, u32[]{:S(2)}) copy-start(bf16[768,2048]{1,0:T(8,128)(2,1)} %ws2.1) | copy-start | bytes 9437188

commit v7 on v6

--- a/solution.py
+++ b/solution.py
@@ -283,12 +283,6 @@
         slot = 2 * others[i] + cx
         table(pk, slot, (others[i], cx), i).wait_recv()
         table(pka.at[slot], slot, partner, 4 + i).start()
-    for i in range(3):
-        slot = 2 * others[i] + cx
-        table(pka.at[slot], slot, partner, 4 + i).wait()
-        table(pk, me, (others[i], cx), i).wait_send()
-    table(pk, me, partner, 3).wait()
-
     def tables():
         tmap[...] = jnp.concatenate([pka[k, :, 0:blk] for k in range(8)], axis=1)
         ids = (me * ne + lax.broadcasted_iota(jnp.int32, (ne, ntok), 0)).astype(F32)
@@ -335,11 +329,16 @@
         slot, dev = relay[k]
         return part(ua.at[slot, rows(k)], slot, k, (dev, cx), s_sem, r_sem, 2)
 
-    tables()
     take(sy, 0, (yn, cx), 1)
     across(0).start()
     take(sx, 1, (xn, cx), 0)
     across(1).start()
+    for i in range(3):
+        slot = 2 * others[i] + cx
+        table(pka.at[slot], slot, partner, 4 + i).wait()
+        table(pk, me, (others[i], cx), i).wait_send()
+    table(pk, me, partner, 3).wait()
+    tables()
     take(sy, 1, (yn, cx), 1)
     take(sx, 0, (xn, cx), 0)
     for k in range(2):

time: 108 us -> 108 us (level)
  no operation moved by 1% of the time
where the time goes in v7:
time: 108 us
  Pallas kernels  107 us (99%)
    pallas_call x1, Pallas kernels, _experts(): pl.pallas_call(_expert_kernel, name='experts', out_shape=(pltpu.VMEM(((nt...  39.3 us
    pallas_call x1, Pallas kernels, _return(): pl.pallas_call(_return_kernel, name='giveback', out_shape=jax.ShapeDtypeS...  29.9 us
    pallas_call x1, Pallas kernels, _attention(): pl.pallas_call(_attn_kernel, name='attn', out_shape=(pltpu.VMEM((b, d), B...  23.3 us
    pallas_call x1, Pallas kernels, _all_gather(): pl.pallas_call(_gather_kernel, name='gather', out_shape=(pltpu.VMEM((8, b...  15 us

profile of v7, /device:TPU:0, one launch (start us, length us, event | category | flops | bytes accessed | tf_op | source)
XLA Modules:
  0.0 108.2 jit_solution(3403082110018934634)
XLA Ops:
  0.0 23.3 %attn.1 = (bf16[64,2048]{1,0:T(8,128)(2,1)S(1)}, bf16[64,2048]{1,0:T(8,128)(2,1)S(1)}, f32[16,128]{1,0:T(8,128)S(1)}) custom-call(s32[64]{0:T(128)} %lens.1, bf16[64,2048]{1,0:T(8,128)(2,1)} %x.1, bf16[2048]{0:T(1024)(128)(2,1)} %ln1.1, bf16[2048]{0:T(1024)(128)(2,1)} %ln2.1, s32[8,64]{1,0:T(8,128)} %bitcast.8, f32[8,64]{1,0:T(8,128)} %bitcast.9, ...), custom_call_target="tpu_custom_call" | custom-call | tf_op jit(solution)/shard_map/attn/pallas_call | solution.py:176
  23.3 15.0 %gather.1 = (bf16[8,64,2048]{2,1,0:T(8,128)(2,1)S(1)}, s32[16,128]{1,0:T(8,128)S(1)}, f32[16,128]{1,0:T(8,128)S(1)}, f32[512,128]{1,0:T(8,128)S(1)}, bf16[4,2048...) custom-call(bf16[64,2048]{1,0:T(8,128)(2,1)S(1)} %get-tuple-element.16.u, ...), custom_call_target="tpu_custom_call" | custom-call | tf_op jit(solution)/shard_map/gather/pallas_call | solution.py:362
  38.3 0.0 copy-start
  38.3 0.0 copy-start.1
  38.3 0.0 copy-start.2
  38.3 39.3 %experts.1 = (f32[8320,128]{1,0:T(8,128)S(1)}, bf16[4,2048,768]{2,1,0:T(8,128)(2,1)S(1)}, bf16[4,2048,768]{2,1,0:T(8,128)(2,1)S(1)}, bf16[4,768,2048]{2,1,0:T(8,128)(2,1)S(1)}) custom-call(s32[16,128]{1,0:T(8,128)S(1)} %get-tuple-element.18.toks, f32[16,128]{1,0:T(8,128)S(1)} %get-tuple-element.19.wgts, ...), custom_call_target="tpu_custom_call", output_to_operand_aliasing={{1}: (4, {}), {2}: (5, {}), {3}: (6, {})} | custom-call | tf_op jit(solution)/shard_map/experts/pallas_call | solution.py:516
  77.6 0.0 copy-done
  77.6 0.0 copy-done.1
  77.6 0.0 copy-done.2
  77.6 29.9 %giveback.1 = bf16[64,2048]{1,0:T(8,128)(2,1)S(1)} custom-call(f32[8320,128]{1,0:T(8,128)S(1)} %get-tuple-element.25.acc, bf16[64,2048]{1,0:T(8,128)(2,1)S(1)} %get-tuple-element.26.h, bf16[64,2048]{1,0:T(8,128)(2,1)S(1)} %get-tuple-element.16.u, bf16[2048,768]{1,0:T(8,128)(2,1)S(1)} %copy-done, bf16[2048,768]{1,0:T(8,128)(2,1)S(1)} %copy-done.1, ...), custom_call_target="tpu_custom_call" | custom-call | tf_op jit(solution)/shard_map/giveback/pallas_call | solution.py:627
  107.5 0.7 copy.24
Async XLA Ops:
  38.3 39.3 %copy-start = (bf16[2048,768]{1,0:T(8,128)(2,1)S(1)}, bf16[2048,768]{1,0:T(8,128)(2,1)}, u32[]{:S(2)}) copy-start(bf16[2048,768]{1,0:T(8,128)(2,1)} %ws1.1) | copy-start | bytes 9437188
  38.3 39.3 %copy-start.1 = (bf16[2048,768]{1,0:T(8,128)(2,1)S(1)}, bf16[2048,768]{1,0:T(8,128)(2,1)}, u32[]{:S(2)}) copy-start(bf16[2048,768]{1,0:T(8,128)(2,1)} %ws3.1) | copy-start | bytes 9437188
  38.3 39.3 %copy-start.2 = (bf16[768,2048]{1,0:T(8,128)(2,1)S(1)}, bf16[768,2048]{1,0:T(8,128)(2,1)}, u32[]{:S(2)}) copy-start(bf16[768,2048]{1,0:T(8,128)(2,1)} %ws2.1) | copy-start | bytes 9437188

commit v8 on v7

--- a/solution.py
+++ b/solution.py
@@ -219,6 +219,7 @@
 
 WBUF = 4
 TILE = 128
+WIDE = 256
 SMALL = 64
 LANES = 16
 PITCH = 17
@@ -425,16 +426,16 @@
     lax.fori_loop(0, ntok * LANES // 256, zero, 0)
     acc[ntok * LANES:, :] = jnp.zeros((STEP8 * LANES, 128), F32)
 
-    def hidden(slot, m):
+    def hidden(slot, m, x):
         for c in range(f // fc):
             s = slice(c * fc, (c + 1) * fc)
-            z1 = jnp.dot(xt[0:m, :], b1[slot, :, s], preferred_element_type=F32)
-            z3 = jnp.dot(xt[0:m, :], b3[slot, :, s], preferred_element_type=F32)
+            z1 = jnp.dot(x(), b1[slot, :, s], preferred_element_type=F32)
+            z3 = jnp.dot(x(), b3[slot, :, s], preferred_element_type=F32)
             gt[0:m, s] = _silu_mul(z1, z3)
 
-    def results(slot, m):
+    def results(slot, m, at0):
         for c in range(d // dc):
-            y = jnp.dot(gt[0:m, :], b2[slot, :, c * dc:(c + 1) * dc], preferred_element_type=F32)
+            y = jnp.dot(gt[at0:at0 + m, :], b2[slot, :, c * dc:(c + 1) * dc], preferred_element_type=F32)
             y = y.astype(BF16).astype(F32)
             for j in range(dc // 128):
                 r3[pl.ds(c * (dc // 128) + j, m, stride=PITCH), :] = y[:, j * 128:(j + 1) * 128]
@@ -455,8 +456,7 @@
                 c.wait()
         n = toks[e, 127]
 
-        @pl.when((n > 0) & (n <= SMALL))
-        def _():
+        def small(size):
             steps = (n + STEP8 - 1) // STEP8
 
             def fetch(i, _):
@@ -466,9 +466,9 @@
                 return 0
             lax.fori_loop(0, steps, fetch, 0)
             for c in range(LANES):
-                xt[0:SMALL, c * 128:(c + 1) * 128] = x3[pl.ds(c, SMALL, stride=PITCH), :].astype(BF16)
-            hidden(slot, SMALL)
-            results(slot, SMALL)
+                xt[0:size, c * 128:(c + 1) * 128] = x3[pl.ds(c, size, stride=PITCH), :].astype(BF16)
+            hidden(slot, size, lambda: xt[0:size, :])
+            results(slot, size, 0)
 
             def add(i, _):
                 where = [at(toks[e, i * STEP8 + k]) for k in range(STEP8)]
@@ -478,6 +478,9 @@
                 return 0
             lax.fori_loop(0, steps, add, 0)
 
+        pl.when((n > 0) & (n <= SMALL // 2))(lambda: small(SMALL // 2))
+        pl.when((n > SMALL // 2) & (n <= SMALL))(lambda: small(SMALL))
+
         @pl.when(n > SMALL)
         def _():
             lane = lax.broadcasted_iota(jnp.int32, (ntok, 128), 1)
@@ -485,21 +488,21 @@
                 jnp.sum(jnp.where(lane == e, cols[...], 0.0), axis=1, keepdims=True), (ntok, 128))
 
             def dense(t, _):
-                rows = pl.ds(pl.multiple_of(t * TILE, TILE), TILE)
-                xt[...] = ua[rows, :]
-                hidden(slot, TILE)
-                results(slot, TILE)
-
-                def add(i, _):
-                    for k in range(STEP8):
-                        m = i * STEP8 + k
-                        one = at(t * TILE + m)
-                        g = gsc[pl.ds(t * TILE + m, 1), :]
-                        acc[one, :] = acc[one, :] + g * r3[wide(m), :]
-                    return 0
-                lax.fori_loop(0, TILE // STEP8, add, 0)
+                rows = pl.ds(pl.multiple_of(t * WIDE, WIDE), WIDE)
+                hidden(slot, WIDE, lambda: ua[rows, :])
+                for part in range(WIDE // TILE):
+                    results(slot, TILE, part * TILE)
+
+                    def add(i, _):
+                        for k in range(STEP8):
+                            m = i * STEP8 + k
+                            one = at(t * WIDE + part * TILE + m)
+                            g = gsc[pl.ds(t * WIDE + part * TILE + m, 1), :]
+                            acc[one, :] = acc[one, :] + g * r3[wide(m), :]
+                        return 0
+                    lax.fori_loop(0, TILE // STEP8, add, 0)
                 return 0
-            lax.fori_loop(0, ntok // TILE, dense, 0)
+            lax.fori_loop(0, ntok // WIDE, dense, 0)
 
         @pl.when(step + WBUF < ne)
         def _():
@@ -527,8 +530,8 @@
             pltpu.VMEM(((ntok + STEP8) * PITCH, 128), F32),
             pltpu.VMEM((SMALL * PITCH, 128), F32),
             pltpu.VMEM((TILE * PITCH, 128), F32),
-            pltpu.VMEM((TILE, d), BF16),
-            pltpu.VMEM((TILE, f), BF16),
+            pltpu.VMEM((SMALL, d), BF16),
+            pltpu.VMEM((WIDE, f), BF16),
             pltpu.VMEM((ntok, 128), F32),
             pltpu.SMEM((ne,), jnp.int32),
             pltpu.SMEM((ne,), jnp.int32),

time: 108 us -> 107 us (level)
    pallas_call x1, Pallas kernels: 29.9 us -> 28.7 us  [_return(): pl.pallas_call(_return_kernel, name='giveback', out_shape=jax.ShapeDtypeS...]
where the time goes in v8:
time: 107 us
  Pallas kernels  106 us (99%)
    pallas_call x1, Pallas kernels, _experts(): pl.pallas_call(_expert_kernel, name='experts', out_shape=(pltpu.VMEM(((nt...  39.2 us
    pallas_call x1, Pallas kernels, _return(): pl.pallas_call(_return_kernel, name='giveback', out_shape=jax.ShapeDtypeS...  28.7 us
    pallas_call x1, Pallas kernels, _attention(): pl.pallas_call(_attn_kernel, name='attn', out_shape=(pltpu.VMEM((b, d), B...  23.3 us
    pallas_call x1, Pallas kernels, _all_gather(): pl.pallas_call(_gather_kernel, name='gather', out_shape=(pltpu.VMEM((8, b...  15 us

profile of v8, /device:TPU:0, one launch (start us, length us, event | category | flops | bytes accessed | tf_op | source)
XLA Modules:
  0.0 107.0 jit_solution(779053479352815203)
XLA Ops:
  0.0 23.3 %attn.1 = (bf16[64,2048]{1,0:T(8,128)(2,1)S(1)}, bf16[64,2048]{1,0:T(8,128)(2,1)S(1)}, f32[16,128]{1,0:T(8,128)S(1)}) custom-call(s32[64]{0:T(128)} %lens.1, bf16[64,2048]{1,0:T(8,128)(2,1)} %x.1, bf16[2048]{0:T(1024)(128)(2,1)} %ln1.1, bf16[2048]{0:T(1024)(128)(2,1)} %ln2.1, s32[8,64]{1,0:T(8,128)} %bitcast.8, f32[8,64]{1,0:T(8,128)} %bitcast.9, ...), custom_call_target="tpu_custom_call" | custom-call | tf_op jit(solution)/shard_map/attn/pallas_call | solution.py:176
  23.3 15.0 %gather.1 = (bf16[8,64,2048]{2,1,0:T(8,128)(2,1)S(1)}, s32[16,128]{1,0:T(8,128)S(1)}, f32[16,128]{1,0:T(8,128)S(1)}, f32[512,128]{1,0:T(8,128)S(1)}, bf16[4,2048...) custom-call(bf16[64,2048]{1,0:T(8,128)(2,1)S(1)} %get-tuple-element.16.u, ...), custom_call_target="tpu_custom_call" | custom-call | tf_op jit(solution)/shard_map/gather/pallas_call | solution.py:363
  38.3 0.0 copy-start
  38.3 0.0 copy-start.1
  38.3 0.0 copy-start.2
  38.3 39.2 %experts.1 = (f32[8320,128]{1,0:T(8,128)S(1)}, bf16[4,2048,768]{2,1,0:T(8,128)(2,1)S(1)}, bf16[4,2048,768]{2,1,0:T(8,128)(2,1)S(1)}, bf16[4,768,2048]{2,1,0:T(8,128)(2,1)S(1)}) custom-call(s32[16,128]{1,0:T(8,128)S(1)} %get-tuple-element.18.toks, f32[16,128]{1,0:T(8,128)S(1)} %get-tuple-element.19.wgts, ...), custom_call_target="tpu_custom_call", output_to_operand_aliasing={{1}: (4, {}), {2}: (5, {}), {3}: (6, {})} | custom-call | tf_op jit(solution)/shard_map/experts/pallas_call | solution.py:519
  77.5 0.0 copy-done
  77.5 0.0 copy-done.1
  77.5 0.0 copy-done.2
  77.5 28.7 %giveback.1 = bf16[64,2048]{1,0:T(8,128)(2,1)S(1)} custom-call(f32[8320,128]{1,0:T(8,128)S(1)} %get-tuple-element.25.acc, bf16[64,2048]{1,0:T(8,128)(2,1)S(1)} %get-tuple-element.26.h, bf16[64,2048]{1,0:T(8,128)(2,1)S(1)} %get-tuple-element.16.u, bf16[2048,768]{1,0:T(8,128)(2,1)S(1)} %copy-done, bf16[2048,768]{1,0:T(8,128)(2,1)S(1)} %copy-done.1, ...), custom_call_target="tpu_custom_call" | custom-call | tf_op jit(solution)/shard_map/giveback/pallas_call | solution.py:630
  106.3 0.7 copy.24
Async XLA Ops:
  38.3 39.2 %copy-start = (bf16[2048,768]{1,0:T(8,128)(2,1)S(1)}, bf16[2048,768]{1,0:T(8,128)(2,1)}, u32[]{:S(2)}) copy-start(bf16[2048,768]{1,0:T(8,128)(2,1)} %ws1.1) | copy-start | bytes 9437188
  38.3 39.2 %copy-start.1 = (bf16[2048,768]{1,0:T(8,128)(2,1)S(1)}, bf16[2048,768]{1,0:T(8,128)(2,1)}, u32[]{:S(2)}) copy-start(bf16[2048,768]{1,0:T(8,128)(2,1)} %ws3.1) | copy-start | bytes 9437188
  38.3 39.2 %copy-start.2 = (bf16[768,2048]{1,0:T(8,128)(2,1)S(1)}, bf16[768,2048]{1,0:T(8,128)(2,1)}, u32[]{:S(2)}) copy-start(bf16[768,2048]{1,0:T(8,128)(2,1)} %ws2.1) | copy-start | bytes 9437188
